TPU v7x, 128 devices: a whole 4x4x4 slice. The times are simulated.
128 devices in a mesh: ctx: 16 (over y, x), tp: 8 (over z, core).
Axes of the slice: x: 4, y: 4, z: 4, core: 2. Of those that a mesh axis runs over, the one named last changes fastest.
Arguments:
- hidden: bfloat16 [8, 8192], P(None, 'ctx'), may hold values from -4.8 to 4.8, as said below
- norm_gains: bfloat16 [4, 8192], P(None, 'ctx'), may hold values from 0.5 to 1.5
- w_query: bfloat16 [4, 8192, 8192], P(None, 'ctx', 'tp'), may hold values from -0.0625 to 0.0625
- w_key: bfloat16 [4, 8192, 1024], P(None, 'ctx', 'tp'), may hold values from -0.125 to 0.125
- w_value: bfloat16 [4, 8192, 1024], P(None, 'ctx', 'tp'), may hold values from -0.125 to 0.125
- w_out: bfloat16 [4, 8192, 8192], P(None, 'tp', 'ctx'), may hold values from -0.0625 to 0.0625
- key_cache: bfloat16 [4, 8, 8, 2048, 128], P(None, None, 'tp', 'ctx'), may hold values from -9 to 9
- value_cache: bfloat16 [4, 8, 8, 2048, 128], P(None, None, 'tp', 'ctx'), may hold values from -6 to 6
- lengths: int32 [8], replicated, may hold values from 1 to 2048, 8200 in all
Outputs:
- updated: float32 [8, 8192], P(None, 'ctx')
Inputs may be any that keep to these rules, and one draw needn't show every extreme that they name: Each sequence has lengths[b] valid cache positions 0 .. lengths[b] - 1, between 1 and 2048; the longest sequence has exactly 2048; the new token sits at position lengths[b]. `hidden`: activations of order 0.2; in each block of 512 consecutive features one sequence, chosen at random, has entries four times larger.
All inputs are finite; a program needn't handle non-finite values.
Results may differ from a plain program's by a relative error of at most 0.02.
Values sent between devices are 32-bit elements.
A program may use at most 64 MiB of HBM per device.

v0:
```python
import functools
import math

import jax
import jax.numpy as jnp
from jax import lax
from jax.sharding import Mesh
from jax.sharding import PartitionSpec as P

D = 8192
CTX = ("ctx_0", "ctx_1")


mask_fill = -1e30
norm_eps = 1e-05
rope_base = 500000.0


def over_axes(shard, axes):
    return functools.reduce(lax.psum, axes, shard)


def one_axis_at_a_time(shard, axes):
    for axis in axes:
        shard = lax.pmax(shard, axis)
    return shard


def over_pieces(shard, axis):
    return lax.all_gather(shard, axis).sum(0)


def rotate(vectors, positions):
    width = vectors.shape[-1]
    half_width = width // 2
    exponents = jnp.arange(half_width, dtype=jnp.float32) * (2.0 / width)
    frequency = jnp.exp(-exponents * math.log(rope_base))
    angles = positions.astype(jnp.float32)[:, None] * frequency[None, :]
    cosine = jnp.cos(angles)[:, None, :]
    sine_part = jnp.sin(angles)[:, None, :]
    first_half = vectors[..., :half_width]
    second_half = vectors[..., half_width:]
    return jnp.concatenate(
        [
            first_half * cosine - second_half * sine_part,
            second_half * cosine + first_half * sine_part,
        ],
        axis=-1,
    )


def on_device(hidden, norm_gains, w_query, w_key, w_value, w_out, key_cache, value_cache, lengths):
    stream = hidden.astype(jnp.float32)
    seq_count = hidden.shape[0]
    head_width = key_cache.shape[4]
    location_total = key_cache.shape[3]
    kv_local = key_cache.shape[2]
    query_local = w_query.shape[2] // head_width
    group_size = query_local // kv_local
    logit_multiplier = 1.0 / math.sqrt(head_width)
    positions = lax.axis_index(CTX) * location_total + jnp.arange(location_total, dtype=jnp.int32)
    usable = (positions[None, :] < lengths[:, None])[:, None, None, :]
    for layer_idx in range(w_query.shape[0]):
        local_squares = jnp.sum(stream * stream, axis=1)
        scaled = (stream * norm_gains[layer_idx].astype(jnp.float32)).astype(jnp.bfloat16)
        query_part = jnp.dot(scaled, w_query[layer_idx], preferred_element_type=jnp.float32)
        key_part = jnp.dot(scaled, w_key[layer_idx], preferred_element_type=jnp.float32)
        value_part = jnp.dot(scaled, w_value[layer_idx], preferred_element_type=jnp.float32)
        squares = over_axes(local_squares, CTX)
        raw_query, raw_key, raw_value = (
            over_axes(query_part, CTX),
            over_axes(key_part, CTX),
            over_axes(value_part, CTX),
        )
        reciprocal_value = lax.rsqrt(squares / D + norm_eps)
        query = rotate(
            (raw_query * reciprocal_value[:, None]).reshape(seq_count, query_local, head_width),
            lengths,
        ).astype(jnp.bfloat16)
        fresh_lookup_vector = rotate(
            (raw_key * reciprocal_value[:, None]).reshape(seq_count, kv_local, head_width), lengths
        ).astype(jnp.bfloat16)
        new_value = (
            (raw_value * reciprocal_value[:, None])
            .reshape(seq_count, kv_local, head_width)
            .astype(jnp.bfloat16)
        )
        shared_head_sets = query.reshape(seq_count, kv_local, group_size, head_width)
        scores = (
            jnp.einsum(
                "bkgd,bksd->bkgs",
                shared_head_sets,
                key_cache[layer_idx],
                preferred_element_type=jnp.float32,
            )
            * logit_multiplier
        )
        masked = jnp.where(usable, scores, mask_fill)
        local_max = jnp.max(masked, axis=-1)
        attention_probabilities = jnp.where(usable, jnp.exp(masked - local_max[..., None]), 0.0)
        local_sum = jnp.sum(attention_probabilities, axis=-1)
        local_out = jnp.einsum(
            "bkgs,bksd->bkgd",
            attention_probabilities.astype(jnp.bfloat16),
            value_cache[layer_idx],
            preferred_element_type=jnp.float32,
        )
        largest = one_axis_at_a_time(local_max, CTX)
        factor = jnp.exp(local_max - largest)
        total_sum, total_out = (
            over_axes(local_sum * factor, CTX),
            over_axes(local_out * factor[..., None], CTX),
        )
        self_match_logit = (
            jnp.einsum(
                "uryj,urj->ury",
                shared_head_sets,
                fresh_lookup_vector,
                preferred_element_type=jnp.float32,
            )
            * logit_multiplier
        )
        row_top = jnp.maximum(largest, self_match_logit)
        carried = jnp.exp(largest - row_top)
        fresh = jnp.exp(self_match_logit - row_top)
        fresh_rounded = lax.optimization_barrier(fresh.astype(jnp.bfloat16)).astype(jnp.float32)
        numerator = (
            total_out * carried[..., None]
            + fresh_rounded[..., None] * new_value.astype(jnp.float32)[:, :, None, :]
        )
        denominator = total_sum * carried + fresh
        context = (
            (numerator / denominator[..., None])
            .reshape(seq_count, query_local * head_width)
            .astype(jnp.bfloat16)
        )
        head_part = jnp.dot(context, w_out[layer_idx], preferred_element_type=jnp.float32)
        stream = stream + over_pieces(head_part, "tp")
    return stream


def solution(mesh):
    finer = Mesh(mesh.devices.reshape(4, 4, mesh.shape["tp"]), ("ctx_0", "ctx_1", "tp"))
    return jax.shard_map(
        on_device,
        mesh=finer,
        in_specs=(
            P(None, CTX),
            P(None, CTX),
            P(None, CTX, "tp"),
            P(None, CTX, "tp"),
            P(None, CTX, "tp"),
            P(None, "tp", CTX),
            P(None, None, "tp", CTX, None),
            P(None, None, "tp", CTX, None),
            P(),
        ),
        out_specs=P(None, CTX),
        check_vma=False,
    )
```

profile of v0, /device:TPU:1, one launch (start us, length us, event | category | flops | bytes accessed | tf_op | source)
XLA Modules:
  0.0 402.6 jit_solution(12077693957421392516)
XLA Ops:
  5.5 1.5 fusion.22
  7.0 14.6 %all-reduce.15 = (f32[8,1024]{1,0:T(8,128)S(1)}, f32[8]{0:T(128)S(1)}) all-reduce(f32[8,1024]{1,0:T(8,128)S(1)} %fusion.22, f32[8]{0:T(128)S(1)} %fusion.65), channel_id=1, replica_groups=mesh['ctx_0'=4,'ctx_1'=4,'tp'=8] {'ctx_0'}, use_global_device_ids=true, to_apply=%region_0.0 | all-reduce | flops 8200 | bytes 65600 | tf_op jit(solution)/shard_map/psum | solution.py:20
  21.7 14.0 %all-reduce.7 = (f32[8,1024]{1,0:T(8,128)S(1)}, f32[8]{0:T(128)S(1)}) all-reduce(f32[8,1024]{1,0:T(8,128)S(1)} %get-tuple-element.51, f32[8]{0:T(128)S(1)} %get-tuple-element.52), channel_id=1, replica_groups=mesh['ctx_0'=4,'ctx_1'=4,'tp'=8] {'ctx_1'}, use_global_device_ids=true, to_apply=%region_1.0 | all-reduce | flops 8200 | bytes 65600 | tf_op jit(solution)/shard_map/psum | solution.py:20
  37.1 6.0 %pmax.56 = f32[8,1,8]{2,0,1:T(8,128)S(1)} all-reduce(f32[8,1,8]{2,0,1:T(8,128)S(1)} %bitcast.314), channel_id=1, replica_groups=mesh['ctx_0'=4,'ctx_1'=4,'tp'=8] {'ctx_0'}, use_global_device_ids=true, to_apply=%region_6.0 | all-reduce | flops 64 | bytes 512 | tf_op jit(solution)/shard_map/pmax | solution.py:25
  43.2 6.0 %pmax.57 = f32[8,1,8]{2,0,1:T(8,128)S(1)} all-reduce(f32[8,1,8]{2,0,1:T(8,128)S(1)} %pmax.56), channel_id=1, replica_groups=mesh['ctx_0'=4,'ctx_1'=4,'tp'=8] {'ctx_1'}, use_global_device_ids=true, to_apply=%region_7.0 | all-reduce | flops 64 | bytes 512 | tf_op jit(solution)/shard_map/pmax | solution.py:25
  50.5 12.8 %all-reduce.14 = (f32[8,1,8]{2,0,1:T(8,128)S(1)}, f32[8,128]{1,0:T(8,128)S(1)}, f32[8,128]{1,0:T(8,128)S(1)}, f32[8,1,8,128]{3,2,0,1:T(8,128)S(1)}) all-reduce(f32[8,1,8]{2,0,1:T(8,128)S(1)} %get-tuple-element.88, f32[8,128]{1,0:T(8,128)S(1)} %fusion.46, ...), channel_id=1, replica_groups=mesh['ctx_0'=4,'ctx_1'=4,'tp'=8] {'ctx_0'}, use_global_device_ids=true, to_apply=%region_15.16 | all-reduce | flops 10304 | bytes 82432 | tf_op jit(solution)/shard_map/psum | solution.py:20
  63.3 13.0 %all-reduce.6 = (f32[8,1,8]{2,0,1:T(8,128)S(1)}, f32[8,128]{1,0:T(8,128)S(1)}, f32[8,128]{1,0:T(8,128)S(1)}, f32[8,1,8,128]{3,2,0,1:T(8,128)S(1)}) all-reduce(f32[8,1,8]{2,0,1:T(8,128)S(1)} %get-tuple-element.47, f32[8,128]{1,0:T(8,128)S(1)} %get-tuple-element.48, ...), channel_id=1, replica_groups=mesh['ctx_0'=4,'ctx_1'=4,'tp'=8] {'ctx_1'}, use_global_device_ids=true, to_apply=%region_16.17 | all-reduce | flops 10304 | bytes 82432 | tf_op jit(solution)/shard_map/psum | solution.py:20
  78.4 32.6 %all-gather = f32[64,512]{1,0:T(8,128)S(1)} all-gather(f32[8,512]{1,0:T(8,128)S(1)} %fusion.20), channel_id=2, replica_groups=mesh['ctx_0'=4,'ctx_1'=4,'tp'=8] {'tp'}, dimensions={0}, use_global_device_ids=true | all-gather | bytes 147456 | tf_op jit(solution)/shard_map/all_gather | solution.py:30
  111.4 1.5 fusion.18
  112.9 11.5 %all-reduce.13 = (f32[8,1024]{1,0:T(8,128)S(1)}, f32[8]{0:T(128)S(1)}) all-reduce(f32[8,1024]{1,0:T(8,128)S(1)} %fusion.18, f32[8]{0:T(128)S(1)} %get-tuple-element.67), channel_id=1, replica_groups=mesh['ctx_0'=4,'ctx_1'=4,'tp'=8] {'ctx_0'}, use_global_device_ids=true, to_apply=%region_18.19 | all-reduce | flops 8200 | bytes 65600 | tf_op jit(solution)/shard_map/psum | solution.py:20
  124.4 11.2 %all-reduce.5 = (f32[8,1024]{1,0:T(8,128)S(1)}, f32[8]{0:T(128)S(1)}) all-reduce(f32[8,1024]{1,0:T(8,128)S(1)} %get-tuple-element.45, f32[8]{0:T(128)S(1)} %get-tuple-element.46), channel_id=1, replica_groups=mesh['ctx_0'=4,'ctx_1'=4,'tp'=8] {'ctx_1'}, use_global_device_ids=true, to_apply=%region_19.20 | all-reduce | flops 8200 | bytes 65600 | tf_op jit(solution)/shard_map/psum | solution.py:20
  136.1 7.6 %pmax.58 = f32[8,1,8]{2,0,1:T(8,128)S(1)} all-reduce(f32[8,1,8]{2,0,1:T(8,128)S(1)} %bitcast.315), channel_id=1, replica_groups=mesh['ctx_0'=4,'ctx_1'=4,'tp'=8] {'ctx_0'}, use_global_device_ids=true, to_apply=%region_24.25 | all-reduce | flops 64 | bytes 512 | tf_op jit(solution)/shard_map/pmax | solution.py:25
  143.7 7.6 %pmax.59 = f32[8,1,8]{2,0,1:T(8,128)S(1)} all-reduce(f32[8,1,8]{2,0,1:T(8,128)S(1)} %pmax.58), channel_id=1, replica_groups=mesh['ctx_0'=4,'ctx_1'=4,'tp'=8] {'ctx_1'}, use_global_device_ids=true, to_apply=%region_25.26 | all-reduce | flops 64 | bytes 512 | tf_op jit(solution)/shard_map/pmax | solution.py:25
  151.7 11.5 %all-reduce.12 = (f32[8,1,8]{2,0,1:T(8,128)S(1)}, f32[8,128]{1,0:T(8,128)S(1)}, f32[8,128]{1,0:T(8,128)S(1)}, f32[8,1,8,128]{3,2,0,1:T(8,128)S(1)}) all-reduce(f32[8,1,8]{2,0,1:T(8,128)S(1)} %get-tuple-element.83, f32[8,128]{1,0:T(8,128)S(1)} %fusion.42, ...), channel_id=1, replica_groups=mesh['ctx_0'=4,'ctx_1'=4,'tp'=8] {'ctx_0'}, use_global_device_ids=true, to_apply=%region_33.34 | all-reduce | flops 10304 | bytes 82432 | tf_op jit(solution)/shard_map/psum | solution.py:20
  163.3 11.7 %all-reduce.4 = (f32[8,1,8]{2,0,1:T(8,128)S(1)}, f32[8,128]{1,0:T(8,128)S(1)}, f32[8,128]{1,0:T(8,128)S(1)}, f32[8,1,8,128]{3,2,0,1:T(8,128)S(1)}) all-reduce(f32[8,1,8]{2,0,1:T(8,128)S(1)} %get-tuple-element.41, f32[8,128]{1,0:T(8,128)S(1)} %get-tuple-element.42, ...), channel_id=1, replica_groups=mesh['ctx_0'=4,'ctx_1'=4,'tp'=8] {'ctx_1'}, use_global_device_ids=true, to_apply=%region_34.35 | all-reduce | flops 10304 | bytes 82432 | tf_op jit(solution)/shard_map/psum | solution.py:20
  177.0 29.8 %all-gather.1 = f32[64,512]{1,0:T(8,128)S(1)} all-gather(f32[8,512]{1,0:T(8,128)S(1)} %fusion.16), channel_id=3, replica_groups=mesh['ctx_0'=4,'ctx_1'=4,'tp'=8] {'tp'}, dimensions={0}, use_global_device_ids=true | all-gather | bytes 147456 | tf_op jit(solution)/shard_map/all_gather | solution.py:30
  207.2 1.5 fusion.14
  208.7 12.7 %all-reduce.11 = (f32[8,1024]{1,0:T(8,128)S(1)}, f32[8]{0:T(128)S(1)}) all-reduce(f32[8,1024]{1,0:T(8,128)S(1)} %fusion.14, f32[8]{0:T(128)S(1)} %get-tuple-element.55), channel_id=1, replica_groups=mesh['ctx_0'=4,'ctx_1'=4,'tp'=8] {'ctx_0'}, use_global_device_ids=true, to_apply=%region_36.37 | all-reduce | flops 8200 | bytes 65600 | tf_op jit(solution)/shard_map/psum | solution.py:20
  221.4 12.6 %all-reduce.3 = (f32[8,1024]{1,0:T(8,128)S(1)}, f32[8]{0:T(128)S(1)}) all-reduce(f32[8,1024]{1,0:T(8,128)S(1)} %get-tuple-element.39, f32[8]{0:T(128)S(1)} %get-tuple-element.40), channel_id=1, replica_groups=mesh['ctx_0'=4,'ctx_1'=4,'tp'=8] {'ctx_1'}, use_global_device_ids=true, to_apply=%region_37.38 | all-reduce | flops 8200 | bytes 65600 | tf_op jit(solution)/shard_map/psum | solution.py:20
  234.6 6.1 %pmax.60 = f32[8,1,8]{2,0,1:T(8,128)S(1)} all-reduce(f32[8,1,8]{2,0,1:T(8,128)S(1)} %bitcast.316), channel_id=1, replica_groups=mesh['ctx_0'=4,'ctx_1'=4,'tp'=8] {'ctx_0'}, use_global_device_ids=true, to_apply=%region_42.43 | all-reduce | flops 64 | bytes 512 | tf_op jit(solution)/shard_map/pmax | solution.py:25
  240.7 6.2 %pmax.61 = f32[8,1,8]{2,0,1:T(8,128)S(1)} all-reduce(f32[8,1,8]{2,0,1:T(8,128)S(1)} %pmax.60), channel_id=1, replica_groups=mesh['ctx_0'=4,'ctx_1'=4,'tp'=8] {'ctx_1'}, use_global_device_ids=true, to_apply=%region_43.44 | all-reduce | flops 64 | bytes 512 | tf_op jit(solution)/shard_map/pmax | solution.py:25
  247.3 12.4 %all-reduce.10 = (f32[8,1,8]{2,0,1:T(8,128)S(1)}, f32[8,128]{1,0:T(8,128)S(1)}, f32[8,128]{1,0:T(8,128)S(1)}, f32[8,1,8,128]{3,2,0,1:T(8,128)S(1)}) all-reduce(f32[8,1,8]{2,0,1:T(8,128)S(1)} %get-tuple-element.78, f32[8,128]{1,0:T(8,128)S(1)} %fusion.38, ...), channel_id=1, replica_groups=mesh['ctx_0'=4,'ctx_1'=4,'tp'=8] {'ctx_0'}, use_global_device_ids=true, to_apply=%region_51.52 | all-reduce | flops 10304 | bytes 82432 | tf_op jit(solution)/shard_map/psum | solution.py:20
  259.7 13.2 %all-reduce.2 = (f32[8,1,8]{2,0,1:T(8,128)S(1)}, f32[8,128]{1,0:T(8,128)S(1)}, f32[8,128]{1,0:T(8,128)S(1)}, f32[8,1,8,128]{3,2,0,1:T(8,128)S(1)}) all-reduce(f32[8,1,8]{2,0,1:T(8,128)S(1)} %get-tuple-element.35, f32[8,128]{1,0:T(8,128)S(1)} %get-tuple-element.36, ...), channel_id=1, replica_groups=mesh['ctx_0'=4,'ctx_1'=4,'tp'=8] {'ctx_1'}, use_global_device_ids=true, to_apply=%region_52.53 | all-reduce | flops 10304 | bytes 82432 | tf_op jit(solution)/shard_map/psum | solution.py:20
  274.9 31.2 %all-gather.2 = f32[64,512]{1,0:T(8,128)S(1)} all-gather(f32[8,512]{1,0:T(8,128)S(1)} %fusion.12), channel_id=4, replica_groups=mesh['ctx_0'=4,'ctx_1'=4,'tp'=8] {'tp'}, dimensions={0}, use_global_device_ids=true | all-gather | bytes 147456 | tf_op jit(solution)/shard_map/all_gather | solution.py:30
  306.5 1.5 fusion.10
  308.0 11.5 %all-reduce.9 = (f32[8,1024]{1,0:T(8,128)S(1)}, f32[8]{0:T(128)S(1)}) all-reduce(f32[8,1024]{1,0:T(8,128)S(1)} %fusion.10, f32[8]{0:T(128)S(1)} %get-tuple-element.53), channel_id=1, replica_groups=mesh['ctx_0'=4,'ctx_1'=4,'tp'=8] {'ctx_0'}, use_global_device_ids=true, to_apply=%region_54.55 | all-reduce | flops 8200 | bytes 65600 | tf_op jit(solution)/shard_map/psum | solution.py:20
  319.5 11.2 %all-reduce.1 = (f32[8,1024]{1,0:T(8,128)S(1)}, f32[8]{0:T(128)S(1)}) all-reduce(f32[8,1024]{1,0:T(8,128)S(1)} %get-tuple-element.33, f32[8]{0:T(128)S(1)} %get-tuple-element.34), channel_id=1, replica_groups=mesh['ctx_0'=4,'ctx_1'=4,'tp'=8] {'ctx_1'}, use_global_device_ids=true, to_apply=%region_55.56 | all-reduce | flops 8200 | bytes 65600 | tf_op jit(solution)/shard_map/psum | solution.py:20
  331.2 7.7 %pmax.62 = f32[8,1,8]{2,0,1:T(8,128)S(1)} all-reduce(f32[8,1,8]{2,0,1:T(8,128)S(1)} %bitcast.313), channel_id=1, replica_groups=mesh['ctx_0'=4,'ctx_1'=4,'tp'=8] {'ctx_0'}, use_global_device_ids=true, to_apply=%region_60.61 | all-reduce | flops 64 | bytes 512 | tf_op jit(solution)/shard_map/pmax | solution.py:25
  338.9 7.3 %pmax.63 = f32[8,1,8]{2,0,1:T(8,128)S(1)} all-reduce(f32[8,1,8]{2,0,1:T(8,128)S(1)} %pmax.62), channel_id=1, replica_groups=mesh['ctx_0'=4,'ctx_1'=4,'tp'=8] {'ctx_1'}, use_global_device_ids=true, to_apply=%region_61.62 | all-reduce | flops 64 | bytes 512 | tf_op jit(solution)/shard_map/pmax | solution.py:25
  346.6 11.9 %all-reduce.8 = (f32[8,1,8]{2,0,1:T(8,128)S(1)}, f32[8,128]{1,0:T(8,128)S(1)}, f32[8,128]{1,0:T(8,128)S(1)}, f32[8,1,8,128]{3,2,0,1:T(8,128)S(1)}) all-reduce(f32[8,1,8]{2,0,1:T(8,128)S(1)} %get-tuple-element.73, f32[8,128]{1,0:T(8,128)S(1)} %fusion.34, ...), channel_id=1, replica_groups=mesh['ctx_0'=4,'ctx_1'=4,'tp'=8] {'ctx_0'}, use_global_device_ids=true, to_apply=%region_69.70 | all-reduce | flops 10304 | bytes 82432 | tf_op jit(solution)/shard_map/psum | solution.py:20
  358.4 11.2 %all-reduce = (f32[8,1,8]{2,0,1:T(8,128)S(1)}, f32[8,128]{1,0:T(8,128)S(1)}, f32[8,128]{1,0:T(8,128)S(1)}, f32[8,1,8,128]{3,2,0,1:T(8,128)S(1)}) all-reduce(f32[8,1,8]{2,0,1:T(8,128)S(1)} %get-tuple-element.29, f32[8,128]{1,0:T(8,128)S(1)} %get-tuple-element.30, ...), channel_id=1, replica_groups=mesh['ctx_0'=4,'ctx_1'=4,'tp'=8] {'ctx_1'}, use_global_device_ids=true, to_apply=%region_70.71 | all-reduce | flops 10304 | bytes 82432 | tf_op jit(solution)/shard_map/psum | solution.py:20
  371.7 30.3 %all-gather.3 = f32[64,512]{1,0:T(8,128)S(1)} all-gather(f32[8,512]{1,0:T(8,128)S(1)} %fusion.8), channel_id=5, replica_groups=mesh['ctx_0'=4,'ctx_1'=4,'tp'=8] {'tp'}, dimensions={0}, use_global_device_ids=true | all-gather | bytes 147456 | tf_op jit(solution)/shard_map/all_gather | solution.py:30
  (99 shorter events, 21.1 us)
Async XLA Ops:
  0.0 111.0 %copy-start.4 = (bf16[8,512]{1,0:T(8,128)(2,1)S(1)}, bf16[8,512]{1,0:T(8,128)(2,1)}, u32[]{:S(2)}) copy-start(bf16[8,512]{1,0:T(8,128)(2,1)} %param.9) | copy-start | bytes 24580
  0.0 111.2 %copy-start.2 = (bf16[4,512,128]{2,1,0:T(8,128)(2,1)S(1)}, bf16[4,512,128]{2,1,0:T(8,128)(2,1)}, u32[]{:S(2)}) copy-start(bf16[4,512,128]{2,1,0:T(8,128)(2,1)} %param.13) | copy-start | bytes 1572868
  0.0 111.3 %copy-start.3 = (bf16[4,512,128]{2,1,0:T(8,128)(2,1)S(1)}, bf16[4,512,128]{2,1,0:T(8,128)(2,1)}, u32[]{:S(2)}) copy-start(bf16[4,512,128]{2,1,0:T(8,128)(2,1)} %param.12) | copy-start | bytes 1572868
  0.0 151.5 %copy-start.1 = (bf16[4,8,1,128,128]{4,3,2,1,0:T(8,128)(2,1)S(1)}, bf16[4,8,1,128,128]{4,3,2,1,0:T(8,128)(2,1)}, u32[]{:S(2)}) copy-start(bf16[4,8,1,128,128]{4,3,2,1,0:T(8,128)(2,1)} %param.16) | copy-start | bytes 3145732
  0.0 135.8 %copy-start = (bf16[4,8,1,128,128]{4,3,2,1,0:T(8,128)(2,1)S(1)}, bf16[4,8,1,128,128]{4,3,2,1,0:T(8,128)(2,1)}, u32[]{:S(2)}) copy-start(bf16[4,8,1,128,128]{4,3,2,1,0:T(8,128)(2,1)} %param.15) | copy-start | bytes 3145732
where the time goes:
time: 404 us; the launch traced here: 403 us
  blocking collectives  375 us (93%)
  matrix products  19.7 us (5%)
  other arithmetic  7.17 us (2%)
    psum x16, blocking collectives, over_axes(): return functools.reduce(lax.psum, axes, shard)  197 us
    all_gather x4, blocking collectives, over_pieces(): return lax.all_gather(shard, axis).sum(0)  124 us
    pmax x8, blocking collectives, one_axis_at_a_time(): shard = lax.pmax(shard, axis)  54.4 us

commit v1 on v0

v1 whole, which is shorter than its diff:
```python
import functools
import math

import jax
import jax.numpy as jnp
from jax import lax
from jax.experimental import pallas as pl
from jax.experimental.pallas import tpu as pltpu
from jax.sharding import Mesh
from jax.sharding import PartitionSpec as P

CTX = ("ctx_0", "ctx_1")
MESH = pl.DeviceIdType.MESH
NORM_EPS = 1e-05
ROPE_BASE = 500000.0
MASK_FILL = -1e30
RING = 4
FAR_FIRST = (2, 1, 3)
TP_STEPS = ((2, 0), (2, 1), (1, 0), (1, 1), (3, 0), (3, 1), (0, 1))
FIRST = 768


def kernel(
    layers, batch, heads, width, span, features,
    hidden_hbm, gains_hbm, wq_hbm, wk_hbm, wv_hbm, wo_hbm, kc_hbm, vc_hbm, lengths,
    out_ref,
    hidden_v, gains_v, wqkv, wo, kcat, vcat, diag,
    a1x, a1y, a2y, a2x, b1x, b1y, b2y, b2x, cbuf,
    in_sem, w_sem, a_send, a_recv, c_send, c_recv,
):
    y = lax.axis_index("ctx_0")
    x = lax.axis_index("ctx_1")
    tp = lax.axis_index("tp")
    z, core = tp // 2, lax.rem(tp, 2)
    columns = heads * width
    f32, bf16 = jnp.float32, jnp.bfloat16

    def tp_partner(step, sign=1):
        dz, other = step
        zz = lax.rem(z + (dz if sign > 0 else RING - dz), RING)
        cc = 1 - core if other else core
        return zz * 2 + cc

    barrier = pltpu.get_barrier_semaphore()
    for d in FAR_FIRST:
        pl.semaphore_signal(barrier, inc=1, device_id={"ctx_1": lax.rem(x + d, RING)}, device_id_type=MESH)
        pl.semaphore_signal(barrier, inc=1, device_id={"ctx_0": lax.rem(y + d, RING)}, device_id_type=MESH)
    for step in TP_STEPS:
        pl.semaphore_signal(barrier, inc=1, device_id={"tp": tp_partner(step)}, device_id_type=MESH)

    def weight_copies(l):
        return (
            pltpu.make_async_copy(wq_hbm.at[l], wqkv.at[l, :, pl.ds(0, columns)], w_sem.at[l, 0]),
            pltpu.make_async_copy(wk_hbm.at[l], wqkv.at[l, :, pl.ds(columns, width)], w_sem.at[l, 1]),
            pltpu.make_async_copy(wv_hbm.at[l], wqkv.at[l, :, pl.ds(columns + width, width)], w_sem.at[l, 2]),
        )

    def late_start(l):
        for b in range(batch):
            pltpu.make_async_copy(
                kc_hbm.at[l, b], kcat.at[l, :, pl.ds(b * width, width)], w_sem.at[l, 3]
            ).start()
        pltpu.make_async_copy(vc_hbm.at[l], vcat.at[l], w_sem.at[l, 4]).start()
        pltpu.make_async_copy(wo_hbm.at[l], wo.at[l], w_sem.at[l, 5]).start()

    hidden_copy = pltpu.make_async_copy(hidden_hbm, hidden_v, in_sem.at[0])
    gains_copy = pltpu.make_async_copy(gains_hbm, gains_v, in_sem.at[1])
    hidden_copy.start()
    gains_copy.start()
    for copy in weight_copies(0):
        copy.start()
    late_start(0)
    for l in range(1, layers):
        for copy in weight_copies(l):
            copy.start()
        late_start(l)

    row = lax.broadcasted_iota(jnp.int32, (batch, width), 0)
    lane = lax.broadcasted_iota(jnp.int32, (batch, width), 1)
    half = width // 2
    length = jnp.zeros((batch, width), jnp.int32)
    for b in range(batch):
        length = jnp.where(row == b, lengths[b], length)
    low = lane < half
    exponents = jnp.where(low, lane, lane - half).astype(f32) * (2.0 / width)
    angles = length.astype(f32) * jnp.exp(-exponents * math.log(ROPE_BASE))
    cosine = jnp.cos(angles)
    sine = jnp.where(low, -jnp.sin(angles), jnp.sin(angles))
    usable = (y * RING + x) * span + lane < length
    scale = 1.0 / math.sqrt(width)
    wide_row = lax.broadcasted_iota(jnp.int32, (2 * batch, batch * width), 0)
    wide_col = lax.broadcasted_iota(jnp.int32, (2 * batch, batch * width), 1)
    own_block = jnp.where(lax.rem(wide_row, batch) == wide_col // width, 1.0, 0.0).astype(bf16)
    for part in range(heads // 2):
        diag[pl.ds(part * 2 * batch, 2 * batch), :] = own_block

    def rotate(u):
        return u * cosine + pltpu.roll(u, half, axis=1) * sine

    def spread(tall):
        return jnp.concatenate([tall] * batch, axis=1) * diag[...]

    def ring_copy(buf, l, axis, me, phase, d):
        return pltpu.make_async_remote_copy(
            src_ref=buf.at[l, me], dst_ref=buf.at[l, me],
            send_sem=a_send.at[l, phase, d - 1], recv_sem=a_recv.at[l, phase, d - 1],
            device_id={axis: lax.rem(me + d, RING)}, device_id_type=MESH,
        )

    def ring_start(*args):
        for d in FAR_FIRST:
            ring_copy(*args, d).start()

    def ring_arrive(buf, l, axis, me, phase):
        for d in (1, 3, 2):
            ring_copy(buf, l, axis, me, phase, d).wait_recv()

    def ring_sent(*args):
        for d in FAR_FIRST:
            ring_copy(*args, d).wait_send()

    def tp_copy(l, k):
        return pltpu.make_async_remote_copy(
            src_ref=cbuf.at[l, tp], dst_ref=cbuf.at[l, tp],
            send_sem=c_send.at[l, k], recv_sem=c_recv.at[l, k],
            device_id={"tp": tp_partner(TP_STEPS[k])}, device_id_type=MESH,
        )

    def total(buf, l):
        return (buf[l, 0] + buf[l, 1]) + (buf[l, 2] + buf[l, 3])

    def tile(values, i):
        return values[:, i * width:(i + 1) * width]

    def over_lane(values, i):
        return jnp.broadcast_to(values[:, i:i + 1], (batch, width))

    def merge(buf, l):
        group = heads // 2
        stats = [buf[l, s, :, pl.ds(group * width, width)] for s in range(RING)]
        top = functools.reduce(jnp.maximum, stats)
        shrink = [jnp.exp(t - top) for t in stats]
        sums = functools.reduce(
            jnp.add, [pltpu.roll(e, half, axis=1) * t for e, t in zip(shrink, stats)]
        )
        out = []
        for i in range(group):
            parts = [
                over_lane(shrink[s], i) * buf[l, s, :, pl.ds(i * width, width)] for s in range(RING)
            ]
            out.append((parts[0] + parts[1]) + (parts[2] + parts[3]))
        return out, jnp.where(low, top, sums)

    def finish(buf, l, own, new_value):
        group = heads // 2
        stats = [buf[l, s, :, pl.ds(group * width, width)] for s in range(RING)] + [own]
        top = functools.reduce(jnp.maximum, stats)
        shrink = [jnp.exp(t - top) for t in stats]
        sums = functools.reduce(
            jnp.add, [e * pltpu.roll(t, half, axis=1) for e, t in zip(shrink, stats)]
        )
        share = [e / sums for e in shrink]
        out = []
        for i in range(group):
            parts = [
                over_lane(share[s], i) * buf[l, s, :, pl.ds(i * width, width)] for s in range(RING)
            ] + [over_lane(share[RING], i) * new_value]
            out.append((parts[0] + parts[1]) + (parts[2] + parts[3]) + parts[4])
        return out

    hidden_copy.wait()
    gains_copy.wait()

    def layer(l, stream):
        for copy in weight_copies(l):
            copy.wait()
        gain = gains_v[pl.ds(l, 1), :].astype(f32)
        scaled = (stream * gain).astype(bf16)
        a1x[l, x] = jnp.dot(scaled, wqkv[l, :, pl.ds(0, FIRST)], preferred_element_type=f32)
        if isinstance(l, int) and l == 0:
            pl.semaphore_wait(barrier, 2 * (RING - 1) + len(TP_STEPS))
        ring_start(a1x, l, "ctx_1", x, 0)
        rest = columns + 2 * width - FIRST
        a1y[l, y, :, pl.ds(0, rest)] = jnp.dot(
            scaled, wqkv[l, :, pl.ds(FIRST, rest)], preferred_element_type=f32
        )
        squares = stream * stream
        a1y[l, y, :, pl.ds(rest, width)] = functools.reduce(
            jnp.add, [tile(squares, i) for i in range(features // width)]
        )
        ring_start(a1y, l, "ctx_0", y, 1)

        ring_arrive(a1x, l, "ctx_1", x, 0)
        a2y[l, y] = total(a1x, l)
        ring_start(a2y, l, "ctx_0", y, 2)
        ring_arrive(a1y, l, "ctx_0", y, 1)
        a2x[l, x] = total(a1y, l)
        ring_start(a2x, l, "ctx_1", x, 3)
        ring_arrive(a2y, l, "ctx_0", y, 2)
        ring_arrive(a2x, l, "ctx_1", x, 3)

        raw = jnp.concatenate([total(a2y, l), total(a2x, l)], axis=1)
        mean = jnp.sum(tile(raw, heads + 2), axis=1, keepdims=True) / (RING * RING * features)
        inverse = lax.rsqrt(mean + NORM_EPS)
        query = [rotate(tile(raw, h) * inverse).astype(bf16) for h in range(heads)]
        tall = jnp.concatenate(query, axis=0)
        pltpu.make_async_copy(kcat.at[l], kcat.at[l], w_sem.at[l, 3]).wait()
        scores = lax.dot_general(
            spread(tall), kcat[l], (((1,), (1,)), ((), ())), preferred_element_type=f32
        ) * scale
        zero = jnp.zeros((batch, width), f32)
        stats_first, stats_last = zero, zero
        weights = []
        for h in range(heads):
            masked = jnp.where(usable, scores[h * batch:(h + 1) * batch], MASK_FILL)
            top = jnp.max(masked, axis=1, keepdims=True)
            weight = jnp.where(usable, jnp.exp(masked - top), 0.0)
            amount = jnp.sum(weight, axis=1, keepdims=True)
            weights.append(weight.astype(bf16))
            i = h % (heads // 2)
            if h < heads // 2:
                stats_first = jnp.where(lane == i, top, jnp.where(lane == half + i, amount, stats_first))
            else:
                stats_last = jnp.where(lane == i, top, jnp.where(lane == half + i, amount, stats_last))
        pltpu.make_async_copy(vc_hbm.at[l], vcat.at[l], w_sem.at[l, 4]).wait()
        sums = jnp.dot(
            spread(jnp.concatenate(weights, axis=0)), vcat[l], preferred_element_type=f32
        )
        group = heads // 2
        for i in range(group):
            b1x[l, x, :, pl.ds(i * width, width)] = sums[i * batch:(i + 1) * batch]
        b1x[l, x, :, pl.ds(group * width, width)] = stats_first
        ring_start(b1x, l, "ctx_1", x, 4)
        for i in range(group):
            b1y[l, y, :, pl.ds(i * width, width)] = sums[(group + i) * batch:(group + i + 1) * batch]
        b1y[l, y, :, pl.ds(group * width, width)] = stats_last
        ring_start(b1y, l, "ctx_0", y, 5)

        new_key = rotate(tile(raw, heads) * inverse).astype(bf16).astype(f32)
        new_value = (tile(raw, heads + 1) * inverse).astype(bf16).astype(f32)
        own = []
        for g in range(2):
            packed = jnp.where(lane >= half, 1.0, 0.0)
            for i in range(group):
                match = jnp.sum(query[g * group + i].astype(f32) * new_key, axis=1, keepdims=True)
                packed = jnp.where(lane == i, match * scale, packed)
            own.append(packed)
        ring_sent(a1x, l, "ctx_1", x, 0)
        ring_sent(a1y, l, "ctx_0", y, 1)
        ring_sent(a2y, l, "ctx_0", y, 2)
        ring_sent(a2x, l, "ctx_1", x, 3)

        ring_arrive(b1x, l, "ctx_1", x, 4)
        merged, stats = merge(b1x, l)
        for i in range(group):
            b2y[l, y, :, pl.ds(i * width, width)] = merged[i]
        b2y[l, y, :, pl.ds(group * width, width)] = stats
        ring_start(b2y, l, "ctx_0", y, 6)
        ring_arrive(b1y, l, "ctx_0", y, 5)
        merged, stats = merge(b1y, l)
        for i in range(group):
            b2x[l, x, :, pl.ds(i * width, width)] = merged[i]
        b2x[l, x, :, pl.ds(group * width, width)] = stats
        ring_start(b2x, l, "ctx_1", x, 7)
        pltpu.make_async_copy(wo_hbm.at[l], wo.at[l], w_sem.at[l, 5]).wait()
        ring_arrive(b2y, l, "ctx_0", y, 6)
        context = finish(b2y, l, own[0], new_value)
        ring_arrive(b2x, l, "ctx_1", x, 7)
        context = context + finish(b2x, l, own[1], new_value)
        context = jnp.concatenate(context, axis=1).astype(bf16)
        cbuf[l, tp] = jnp.dot(context, wo[l], preferred_element_type=f32)
        for k in range(len(TP_STEPS)):
            tp_copy(l, k).start()
        ring_sent(b1x, l, "ctx_1", x, 4)
        ring_sent(b1y, l, "ctx_0", y, 5)
        ring_sent(b2y, l, "ctx_0", y, 6)
        ring_sent(b2x, l, "ctx_1", x, 7)
        for k in reversed(range(len(TP_STEPS))):
            tp_copy(l, k).wait_recv()
        parts = [cbuf[l, t] for t in range(2 * RING)]
        stream = stream + (
            ((parts[0] + parts[1]) + (parts[2] + parts[3])) + ((parts[4] + parts[5]) + (parts[6] + parts[7]))
        )
        for k in range(len(TP_STEPS)):
            tp_copy(l, k).wait_send()
        return stream

    stream = hidden_v[...].astype(f32)
    for l in range(layers):
        stream = layer(l, stream)
    out_ref[...] = stream


def on_device(hidden, norm_gains, w_query, w_key, w_value, w_out, key_cache, value_cache, lengths):
    layers, features, columns = w_query.shape
    batch, _, span, width = key_cache.shape[1:]
    heads = columns // width
    keys = key_cache.reshape(layers, batch, span, width)
    values = value_cache.reshape(layers, batch * span, width)
    f32, bf16 = jnp.float32, jnp.bfloat16
    total = columns + 2 * width
    last = total - FIRST + width
    packed = (heads // 2 + 1) * width
    anywhere = pl.BlockSpec(memory_space=pl.ANY)
    return pl.pallas_call(
        functools.partial(kernel, layers, batch, heads, width, span, features),
        out_shape=jax.ShapeDtypeStruct((batch, features), f32),
        in_specs=[anywhere] * 8 + [pl.BlockSpec(memory_space=pltpu.SMEM)],
        out_specs=pl.BlockSpec(memory_space=pltpu.VMEM),
        scratch_shapes=[
            pltpu.VMEM((batch, features), bf16),
            pltpu.VMEM((layers, features), bf16),
            pltpu.VMEM((layers, features, total), bf16),
            pltpu.VMEM((layers, columns, features), bf16),
            pltpu.VMEM((layers, span, batch * width), bf16),
            pltpu.VMEM((layers, batch * span, width), bf16),
            pltpu.VMEM((heads * batch, batch * width), bf16),
            pltpu.VMEM((layers, RING, batch, FIRST), f32),
            pltpu.VMEM((layers, RING, batch, last), f32),
            pltpu.VMEM((layers, RING, batch, FIRST), f32),
            pltpu.VMEM((layers, RING, batch, last), f32),
            pltpu.VMEM((layers, RING, batch, packed), f32),
            pltpu.VMEM((layers, RING, batch, packed), f32),
            pltpu.VMEM((layers, RING, batch, packed), f32),
            pltpu.VMEM((layers, RING, batch, packed), f32),
            pltpu.VMEM((layers, 2 * RING, batch, features), f32),
            pltpu.SemaphoreType.DMA((2,)),
            pltpu.SemaphoreType.DMA((layers, 6)),
            pltpu.SemaphoreType.DMA((layers, 8, RING - 1)),
            pltpu.SemaphoreType.DMA((layers, 8, RING - 1)),
            pltpu.SemaphoreType.DMA((layers, len(TP_STEPS))),
            pltpu.SemaphoreType.DMA((layers, len(TP_STEPS))),
        ],
        compiler_params=pltpu.CompilerParams(
            collective_id=0, has_side_effects=True, vmem_limit_bytes=48 * 1024 * 1024
        ),
    )(hidden, norm_gains, w_query, w_key, w_value, w_out, keys, values, lengths)


def solution(mesh):
    finer = Mesh(mesh.devices.reshape(RING, RING, mesh.shape["tp"]), CTX + ("tp",))
    return jax.shard_map(
        on_device,
        mesh=finer,
        in_specs=(
            P(None, CTX),
            P(None, CTX),
            P(None, CTX, "tp"),
            P(None, CTX, "tp"),
            P(None, CTX, "tp"),
            P(None, "tp", CTX),
            P(None, None, "tp", CTX, None),
            P(None, None, "tp", CTX, None),
            P(),
        ),
        out_specs=P(None, CTX),
        check_vma=False,
    )
```

time: 404 us -> 97.8 us (0.24)
  blocking collectives: 375 us -> 0 us
  Pallas kernels: 0 us -> 90.2 us
  matrix products: 19.7 us -> 0 us
  other arithmetic: 7.17 us -> 0 us
  local copies, waits for them, and re-layouts: 0.13 us -> 7.18 us
    psum x16 -> x0, blocking collectives: 197 us -> none  [over_axes(): return functools.reduce(lax.psum, axes, shard)]
    all_gather x4 -> x0, blocking collectives: 124 us -> none  [over_pieces(): return lax.all_gather(shard, axis).sum(0)]
    pallas_call x0 -> x1, Pallas kernels: none -> 90.2 us  [on_device(): pl.pallas_call(functools.partial(kernel, layers, batch, heads, width, spa...]
    pmax x8 -> x0, blocking collectives: 54.4 us -> none  [one_axis_at_a_time(): shard = lax.pmax(shard, axis)]
    dot_general x28 -> x0, matrix products: 19.7 us -> none  [the longest x4 5.92 us: on_device(): jnp.dot(scaled, w_query[layer_idx], preferred_element_type=jnp.float32)]
    unnamed x13 -> x15, local copies, waits for them, and re-layouts: 0.06 us -> 7.18 us
where the time goes in v1:
time: 97.8 us; the launch traced here: 97.4 us
  Pallas kernels  90.2 us (92%)
  local copies, waits for them, and re-layouts  7.18 us (7%)
    pallas_call x1, Pallas kernels, on_device(): pl.pallas_call(functools.partial(kernel, layers, batch, heads, width, spa...  90.2 us
    unnamed x15, local copies, waits for them, and re-layouts  7.18 us

profile of v1, /device:TPU:1, one launch (start us, length us, event | category | flops | bytes accessed | tf_op | source)
XLA Modules:
  0.0 97.4 jit_solution(16649845379371804693)
XLA Ops:
  0.0 0.0 copy-start
  0.0 1.2 %copy-done = bf16[4,8,1,128,128]{4,3,2,1,0:T(8,128)(2,1)S(1)} copy-done((bf16[4,8,1,128,128]{4,3,2,1,0:T(8,128)(2,1)S(1)}, bf16[4,8,1,128,128]{4,3,2,1,0:T(8,128)(2,1)}, u32[]{:S(2)}) %copy-start) | copy-done | bytes 1048600
  1.2 0.0 copy-start.1
  1.2 1.2 %copy-done.1 = bf16[4,8,1,128,128]{4,3,2,1,0:T(8,128)(2,1)S(1)} copy-done((bf16[4,8,1,128,128]{4,3,2,1,0:T(8,128)(2,1)S(1)}, bf16[4,8,1,128,128]{4,3,2,1,0:T(8,128)(2,1)}, u32[]{:S(2)}) %copy-start.1) | copy-done | bytes 1048600
  2.5 0.0 copy-start.2
  2.5 1.0 %copy-done.2 = bf16[4,512,128]{2,1,0:T(8,128)(2,1)S(1)} copy-done((bf16[4,512,128]{2,1,0:T(8,128)(2,1)S(1)}, bf16[4,512,128]{2,1,0:T(8,128)(2,1)}, u32[]{:S(2)}) %copy-start.2) | copy-done | bytes 524312
  3.5 0.0 copy-start.3
  3.5 1.0 %copy-done.3 = bf16[4,512,128]{2,1,0:T(8,128)(2,1)S(1)} copy-done((bf16[4,512,128]{2,1,0:T(8,128)(2,1)S(1)}, bf16[4,512,128]{2,1,0:T(8,128)(2,1)}, u32[]{:S(2)}) %copy-start.3) | copy-done | bytes 524312
  4.5 0.0 copy-start.4
  4.5 0.7 copy-done.4
  5.2 0.0 copy-start.5
  5.2 0.7 copy-done.5
  5.9 0.0 copy-start.6
  5.9 0.7 copy-done.6
  6.6 90.2 %shard_map.91 = f32[8,512]{1,0:T(8,128)S(1)} custom-call(bf16[8,512]{1,0:T(8,128)(2,1)S(1)} %copy-done.4, bf16[4,512]{1,0:T(4,128)(2,1)S(1)} %copy-done.5, bf16[4,512,1024]{2,1,0:T(8,128)(2,1)} %wq_hbm.1, bf16[4,512,128]{2,1,0:T(8,128)(2,1)S(1)} %copy-done.2, bf16[4,512,128]{2,1,0:T(8,128)(2,1)S(1)} %copy-done.3, bf16[4,1024,512]{2,1,0:T(8,128)(2,1)} %wo_hbm.1, ...), custom_call_target="tpu_custom_call" | custom-call | tf_op jit(solution)/shard_map/pallas_call | solution.py:305
  96.8 0.6 copy.11
Async XLA Ops:
  0.0 1.2 %copy-start = (bf16[4,8,1,128,128]{4,3,2,1,0:T(8,128)(2,1)S(1)}, bf16[4,8,1,128,128]{4,3,2,1,0:T(8,128)(2,1)}, u32[]{:S(2)}) copy-start(bf16[4,8,1,128,128]{4,3,2,1,0:T(8,128)(2,1)} %param.15) | copy-start | bytes 3145732
  1.2 1.2 %copy-start.1 = (bf16[4,8,1,128,128]{4,3,2,1,0:T(8,128)(2,1)S(1)}, bf16[4,8,1,128,128]{4,3,2,1,0:T(8,128)(2,1)}, u32[]{:S(2)}) copy-start(bf16[4,8,1,128,128]{4,3,2,1,0:T(8,128)(2,1)} %param.16) | copy-start | bytes 3145732
  2.5 1.0 %copy-start.2 = (bf16[4,512,128]{2,1,0:T(8,128)(2,1)S(1)}, bf16[4,512,128]{2,1,0:T(8,128)(2,1)}, u32[]{:S(2)}) copy-start(bf16[4,512,128]{2,1,0:T(8,128)(2,1)} %wk_hbm.1) | copy-start | bytes 1572868
  3.5 1.0 %copy-start.3 = (bf16[4,512,128]{2,1,0:T(8,128)(2,1)S(1)}, bf16[4,512,128]{2,1,0:T(8,128)(2,1)}, u32[]{:S(2)}) copy-start(bf16[4,512,128]{2,1,0:T(8,128)(2,1)} %wv_hbm.1) | copy-start | bytes 1572868
  4.5 0.7 copy-start.4
  5.2 0.7 copy-start.5
  5.9 0.7 copy-start.6

commit v2 on v1

--- a/solution.py
+++ b/solution.py
@@ -15,17 +15,18 @@
 ROPE_BASE = 500000.0
 MASK_FILL = -1e30
 RING = 4
-FAR_FIRST = (2, 1, 3)
+FAR_FIRST = (2, 1, 3, 0)
 TP_STEPS = ((2, 0), (2, 1), (1, 0), (1, 1), (3, 0), (3, 1), (0, 1))
 FIRST = 768
 
 
 def kernel(
     layers, batch, heads, width, span, features,
-    hidden_hbm, gains_hbm, wq_hbm, wk_hbm, wv_hbm, wo_hbm, kc_hbm, vc_hbm, lengths,
+    hidden_hbm, gains_hbm, wq_hbm, wk_hbm, wv_hbm, wo_hbm, kc_hbm, vc_hbm, lengths_hbm,
     out_ref,
-    hidden_v, gains_v, wqkv, wo, kcat, vcat, diag,
-    a1x, a1y, a2y, a2x, b1x, b1y, b2y, b2x, cbuf,
+    lengths, hidden_v, gains_v, wqkv, wo, kcat, vcat, diag,
+    a1x, a1y, a2y, a2x, b1x, b1y, b2y, b2x,
+    a1xo, a1yo, a2yo, a2xo, b1xo, b1yo, b2yo, b2xo, cbuf,
     in_sem, w_sem, a_send, a_recv, c_send, c_recv,
 ):
     y = lax.axis_index("ctx_0")
@@ -42,9 +43,14 @@
         return zz * 2 + cc
 
     barrier = pltpu.get_barrier_semaphore()
-    for d in FAR_FIRST:
-        pl.semaphore_signal(barrier, inc=1, device_id={"ctx_1": lax.rem(x + d, RING)}, device_id_type=MESH)
-        pl.semaphore_signal(barrier, inc=1, device_id={"ctx_0": lax.rem(y + d, RING)}, device_id_type=MESH)
+    swapped = tp + 1 - 2 * core
+    for d in FAR_FIRST[:-1]:
+        pl.semaphore_signal(
+            barrier, inc=1, device_id={"ctx_1": lax.rem(x + d, RING), "tp": swapped}, device_id_type=MESH
+        )
+        pl.semaphore_signal(
+            barrier, inc=1, device_id={"ctx_0": lax.rem(y + d, RING), "tp": swapped}, device_id_type=MESH
+        )
     for step in TP_STEPS:
         pl.semaphore_signal(barrier, inc=1, device_id={"tp": tp_partner(step)}, device_id_type=MESH)
 
@@ -65,16 +71,14 @@
 
     hidden_copy = pltpu.make_async_copy(hidden_hbm, hidden_v, in_sem.at[0])
     gains_copy = pltpu.make_async_copy(gains_hbm, gains_v, in_sem.at[1])
+    lengths_copy = pltpu.make_async_copy(lengths_hbm, lengths, in_sem.at[2])
+    lengths_copy.start()
     hidden_copy.start()
     gains_copy.start()
     for copy in weight_copies(0):
         copy.start()
-    late_start(0)
-    for l in range(1, layers):
-        for copy in weight_copies(l):
-            copy.start()
-        late_start(l)
-
+
+    lengths_copy.wait()
     row = lax.broadcasted_iota(jnp.int32, (batch, width), 0)
     lane = lax.broadcasted_iota(jnp.int32, (batch, width), 1)
     half = width // 2
@@ -100,20 +104,24 @@
     def spread(tall):
         return jnp.concatenate([tall] * batch, axis=1) * diag[...]
 
-    def ring_copy(buf, l, axis, me, phase, d):
+    def ring_copy(out, buf, l, axis, me, phase, d):
         return pltpu.make_async_remote_copy(
-            src_ref=buf.at[l, me], dst_ref=buf.at[l, me],
-            send_sem=a_send.at[l, phase, d - 1], recv_sem=a_recv.at[l, phase, d - 1],
-            device_id={axis: lax.rem(me + d, RING)}, device_id_type=MESH,
+            src_ref=out.at[l], dst_ref=buf.at[l, me],
+            send_sem=a_send.at[l, phase, d], recv_sem=a_recv.at[l, phase, d],
+            device_id={axis: lax.rem(me + d, RING), "tp": swapped}, device_id_type=MESH,
         )
 
     def ring_start(*args):
         for d in FAR_FIRST:
             ring_copy(*args, d).start()
 
-    def ring_arrive(buf, l, axis, me, phase):
-        for d in (1, 3, 2):
-            ring_copy(buf, l, axis, me, phase, d).wait_recv()
+    def ring_arrive(out, buf, l, axis, me, phase):
+        for d in reversed(FAR_FIRST):
+            pltpu.make_async_remote_copy(
+                src_ref=out.at[l], dst_ref=buf.at[l, lax.rem(me + RING - d, RING)],
+                send_sem=a_send.at[l, phase, d], recv_sem=a_recv.at[l, phase, d],
+                device_id={axis: lax.rem(me + d, RING), "tp": swapped}, device_id_type=MESH,
+            ).wait_recv()
 
     def ring_sent(*args):
         for d in FAR_FIRST:
@@ -174,30 +182,36 @@
     def layer(l, stream):
         for copy in weight_copies(l):
             copy.wait()
+        if l == 0:
+            late_start(0)
+            for later in range(1, layers):
+                for copy in weight_copies(later):
+                    copy.start()
+                late_start(later)
         gain = gains_v[pl.ds(l, 1), :].astype(f32)
         scaled = (stream * gain).astype(bf16)
-        a1x[l, x] = jnp.dot(scaled, wqkv[l, :, pl.ds(0, FIRST)], preferred_element_type=f32)
-        if isinstance(l, int) and l == 0:
+        a1xo[l] = jnp.dot(scaled, wqkv[l, :, pl.ds(0, FIRST)], preferred_element_type=f32)
+        if l == 0:
             pl.semaphore_wait(barrier, 2 * (RING - 1) + len(TP_STEPS))
-        ring_start(a1x, l, "ctx_1", x, 0)
+        ring_start(a1xo, a1x, l, "ctx_1", x, 0)
         rest = columns + 2 * width - FIRST
-        a1y[l, y, :, pl.ds(0, rest)] = jnp.dot(
+        a1yo[l, :, pl.ds(0, rest)] = jnp.dot(
             scaled, wqkv[l, :, pl.ds(FIRST, rest)], preferred_element_type=f32
         )
         squares = stream * stream
-        a1y[l, y, :, pl.ds(rest, width)] = functools.reduce(
+        a1yo[l, :, pl.ds(rest, width)] = functools.reduce(
             jnp.add, [tile(squares, i) for i in range(features // width)]
         )
-        ring_start(a1y, l, "ctx_0", y, 1)
-
-        ring_arrive(a1x, l, "ctx_1", x, 0)
-        a2y[l, y] = total(a1x, l)
-        ring_start(a2y, l, "ctx_0", y, 2)
-        ring_arrive(a1y, l, "ctx_0", y, 1)
-        a2x[l, x] = total(a1y, l)
-        ring_start(a2x, l, "ctx_1", x, 3)
-        ring_arrive(a2y, l, "ctx_0", y, 2)
-        ring_arrive(a2x, l, "ctx_1", x, 3)
+        ring_start(a1yo, a1y, l, "ctx_0", y, 1)
+
+        ring_arrive(a1xo, a1x, l, "ctx_1", x, 0)
+        a2yo[l] = total(a1x, l)
+        ring_start(a2yo, a2y, l, "ctx_0", y, 2)
+        ring_arrive(a1yo, a1y, l, "ctx_0", y, 1)
+        a2xo[l] = total(a1y, l)
+        ring_start(a2xo, a2x, l, "ctx_1", x, 3)
+        ring_arrive(a2yo, a2y, l, "ctx_0", y, 2)
+        ring_arrive(a2xo, a2x, l, "ctx_1", x, 3)
 
         raw = jnp.concatenate([total(a2y, l), total(a2x, l)], axis=1)
         mean = jnp.sum(tile(raw, heads + 2), axis=1, keepdims=True) / (RING * RING * features)
@@ -228,13 +242,13 @@
         )
         group = heads // 2
         for i in range(group):
-            b1x[l, x, :, pl.ds(i * width, width)] = sums[i * batch:(i + 1) * batch]
-        b1x[l, x, :, pl.ds(group * width, width)] = stats_first
-        ring_start(b1x, l, "ctx_1", x, 4)
-        for i in range(group):
-            b1y[l, y, :, pl.ds(i * width, width)] = sums[(group + i) * batch:(group + i + 1) * batch]
-        b1y[l, y, :, pl.ds(group * width, width)] = stats_last
-        ring_start(b1y, l, "ctx_0", y, 5)
+            b1xo[l, :, pl.ds(i * width, width)] = sums[i * batch:(i + 1) * batch]
+        b1xo[l, :, pl.ds(group * width, width)] = stats_first
+        ring_start(b1xo, b1x, l, "ctx_1", x, 4)
+        for i in range(group):
+            b1yo[l, :, pl.ds(i * width, width)] = sums[(group + i) * batch:(group + i + 1) * batch]
+        b1yo[l, :, pl.ds(group * width, width)] = stats_last
+        ring_start(b1yo, b1y, l, "ctx_0", y, 5)
 
         new_key = rotate(tile(raw, heads) * inverse).astype(bf16).astype(f32)
         new_value = (tile(raw, heads + 1) * inverse).astype(bf16).astype(f32)
@@ -245,36 +259,36 @@
                 match = jnp.sum(query[g * group + i].astype(f32) * new_key, axis=1, keepdims=True)
                 packed = jnp.where(lane == i, match * scale, packed)
             own.append(packed)
-        ring_sent(a1x, l, "ctx_1", x, 0)
-        ring_sent(a1y, l, "ctx_0", y, 1)
-        ring_sent(a2y, l, "ctx_0", y, 2)
-        ring_sent(a2x, l, "ctx_1", x, 3)
-
-        ring_arrive(b1x, l, "ctx_1", x, 4)
+        ring_sent(a1xo, a1x, l, "ctx_1", x, 0)
+        ring_sent(a1yo, a1y, l, "ctx_0", y, 1)
+        ring_sent(a2yo, a2y, l, "ctx_0", y, 2)
+        ring_sent(a2xo, a2x, l, "ctx_1", x, 3)
+
+        ring_arrive(b1xo, b1x, l, "ctx_1", x, 4)
         merged, stats = merge(b1x, l)
         for i in range(group):
-            b2y[l, y, :, pl.ds(i * width, width)] = merged[i]
-        b2y[l, y, :, pl.ds(group * width, width)] = stats
-        ring_start(b2y, l, "ctx_0", y, 6)
-        ring_arrive(b1y, l, "ctx_0", y, 5)
+            b2yo[l, :, pl.ds(i * width, width)] = merged[i]
+        b2yo[l, :, pl.ds(group * width, width)] = stats
+        ring_start(b2yo, b2y, l, "ctx_0", y, 6)
+        ring_arrive(b1yo, b1y, l, "ctx_0", y, 5)
         merged, stats = merge(b1y, l)
         for i in range(group):
-            b2x[l, x, :, pl.ds(i * width, width)] = merged[i]
-        b2x[l, x, :, pl.ds(group * width, width)] = stats
-        ring_start(b2x, l, "ctx_1", x, 7)
+            b2xo[l, :, pl.ds(i * width, width)] = merged[i]
+        b2xo[l, :, pl.ds(group * width, width)] = stats
+        ring_start(b2xo, b2x, l, "ctx_1", x, 7)
         pltpu.make_async_copy(wo_hbm.at[l], wo.at[l], w_sem.at[l, 5]).wait()
-        ring_arrive(b2y, l, "ctx_0", y, 6)
+        ring_arrive(b2yo, b2y, l, "ctx_0", y, 6)
         context = finish(b2y, l, own[0], new_value)
-        ring_arrive(b2x, l, "ctx_1", x, 7)
+        ring_arrive(b2xo, b2x, l, "ctx_1", x, 7)
         context = context + finish(b2x, l, own[1], new_value)
         context = jnp.concatenate(context, axis=1).astype(bf16)
         cbuf[l, tp] = jnp.dot(context, wo[l], preferred_element_type=f32)
         for k in range(len(TP_STEPS)):
             tp_copy(l, k).start()
-        ring_sent(b1x, l, "ctx_1", x, 4)
-        ring_sent(b1y, l, "ctx_0", y, 5)
-        ring_sent(b2y, l, "ctx_0", y, 6)
-        ring_sent(b2x, l, "ctx_1", x, 7)
+        ring_sent(b1xo, b1x, l, "ctx_1", x, 4)
+        ring_sent(b1yo, b1y, l, "ctx_0", y, 5)
+        ring_sent(b2yo, b2y, l, "ctx_0", y, 6)
+        ring_sent(b2xo, b2x, l, "ctx_1", x, 7)
         for k in reversed(range(len(TP_STEPS))):
             tp_copy(l, k).wait_recv()
         parts = [cbuf[l, t] for t in range(2 * RING)]
@@ -301,13 +315,14 @@
     total = columns + 2 * width
     last = total - FIRST + width
     packed = (heads // 2 + 1) * width
-    anywhere = pl.BlockSpec(memory_space=pl.ANY)
+    messages = (FIRST, last, FIRST, last, packed, packed, packed, packed)
     return pl.pallas_call(
         functools.partial(kernel, layers, batch, heads, width, span, features),
         out_shape=jax.ShapeDtypeStruct((batch, features), f32),
-        in_specs=[anywhere] * 8 + [pl.BlockSpec(memory_space=pltpu.SMEM)],
+        in_specs=[pl.BlockSpec(memory_space=pltpu.HBM)] * 9,
         out_specs=pl.BlockSpec(memory_space=pltpu.VMEM),
         scratch_shapes=[
+            pltpu.SMEM((batch,), jnp.int32),
             pltpu.VMEM((batch, features), bf16),
             pltpu.VMEM((layers, features), bf16),
             pltpu.VMEM((layers, features, total), bf16),
@@ -315,26 +330,20 @@
             pltpu.VMEM((layers, span, batch * width), bf16),
             pltpu.VMEM((layers, batch * span, width), bf16),
             pltpu.VMEM((heads * batch, batch * width), bf16),
-            pltpu.VMEM((layers, RING, batch, FIRST), f32),
-            pltpu.VMEM((layers, RING, batch, last), f32),
-            pltpu.VMEM((layers, RING, batch, FIRST), f32),
-            pltpu.VMEM((layers, RING, batch, last), f32),
-            pltpu.VMEM((layers, RING, batch, packed), f32),
-            pltpu.VMEM((layers, RING, batch, packed), f32),
-            pltpu.VMEM((layers, RING, batch, packed), f32),
-            pltpu.VMEM((layers, RING, batch, packed), f32),
+            *[pltpu.VMEM((layers, RING, batch, w), f32) for w in messages],
+            *[pltpu.VMEM((layers, batch, w), f32) for w in messages],
             pltpu.VMEM((layers, 2 * RING, batch, features), f32),
-            pltpu.SemaphoreType.DMA((2,)),
+            pltpu.SemaphoreType.DMA((3,)),
             pltpu.SemaphoreType.DMA((layers, 6)),
-            pltpu.SemaphoreType.DMA((layers, 8, RING - 1)),
-            pltpu.SemaphoreType.DMA((layers, 8, RING - 1)),
+            pltpu.SemaphoreType.DMA((layers, 8, RING)),
+            pltpu.SemaphoreType.DMA((layers, 8, RING)),
             pltpu.SemaphoreType.DMA((layers, len(TP_STEPS))),
             pltpu.SemaphoreType.DMA((layers, len(TP_STEPS))),
         ],
         compiler_params=pltpu.CompilerParams(
             collective_id=0, has_side_effects=True, vmem_limit_bytes=48 * 1024 * 1024
         ),
-    )(hidden, norm_gains, w_query, w_key, w_value, w_out, keys, values, lengths)
+    )(*[pltpu.with_memory_space_constraint(a, pltpu.HBM) for a in (hidden, norm_gains, w_query, w_key, w_value, w_out, keys, values, lengths)])
 
 
 def solution(mesh):

time: 97.8 us -> 87.5 us (0.89)
  local copies, waits for them, and re-layouts: 7.18 us -> 0.61 us
  Pallas kernels: 90.2 us -> 86.8 us
    unnamed x15 -> x1, local copies, waits for them, and re-layouts: 7.18 us -> 0.61 us
    pallas_call x1, Pallas kernels: 90.2 us -> 86.8 us  [on_device(): pl.pallas_call(functools.partial(kernel, layers, batch, heads, width, spa...]
where the time goes in v2:
time: 87.5 us; the launch traced here: 87.4 us
  Pallas kernels  86.8 us (99%)
    pallas_call x1, Pallas kernels, on_device(): pl.pallas_call(functools.partial(kernel, layers, batch, heads, width, spa...  86.8 us

profile of v2, /device:TPU:1, one launch (start us, length us, event | category | flops | bytes accessed | tf_op | source)
XLA Modules:
  0.0 87.4 jit_solution(15526709240404211596)
XLA Ops:
  0.0 86.8 %shard_map.91 = f32[8,512]{1,0:T(8,128)S(1)} custom-call(bf16[8,512]{1,0:T(8,128)(2,1)} %hidden_hbm.1, bf16[4,512]{1,0:T(4,128)(2,1)} %gains_hbm.1, bf16[4,512,1024]{2,1,0:T(8,128)(2,1)} %wq_hbm.1, bf16[4,512,128]{2,1,0:T(8,128)(2,1)} %wk_hbm.1, bf16[4,512,128]{2,1,0:T(8,128)(2,1)} %wv_hbm.1, bf16[4,1024,512]{2,1,0:T(8,128)(2,1)} %wo_hbm.1, ...), custom_call_target="tpu_custom_call" | custom-call | tf_op jit(solution)/shard_map/pallas_call | solution.py:319
  86.8 0.6 copy.11

commit v3 on v2

v3 whole, which is shorter than its diff:
```python
import functools
import math

import jax
import jax.numpy as jnp
from jax import lax
from jax.experimental import pallas as pl
from jax.experimental.pallas import tpu as pltpu
from jax.sharding import Mesh
from jax.sharding import PartitionSpec as P

CTX = ("ctx_0", "ctx_1")
MESH = pl.DeviceIdType.MESH
NORM_EPS = 1e-05
ROPE_BASE = 500000.0
MASK_FILL = -1e30
RING = 4
FAR_FIRST = (2, 1, 3, 0)
TP_STEPS = ((2, 0), (2, 1), (1, 0), (1, 1), (3, 0), (3, 1), (0, 1))
A_PARTS = ((True, (0, 1), 1), (False, (4, 5), 0), (True, (2, 3), 0), (False, (6, 7), 0), (False, (8, 9), 0))
B_PARTS = ((True, (0, 1), 1), (False, (4, 5), 1), (True, (2, 3), 0), (False, (6, 7), 0))
PARTS = A_PARTS + B_PARTS
C_PARTS = 2


def kernel(
    layers, batch, heads, width, span, features,
    hidden_hbm, gains_hbm, wq_hbm, wk_hbm, wv_hbm, wo_hbm, kc_hbm, vc_hbm, lengths_hbm,
    out_ref,
    lengths, hidden_v, gains_v, wqkv, wo, kcat, vcat, diag,
    *rest,
):
    y = lax.axis_index("ctx_0")
    x = lax.axis_index("ctx_1")
    tp = lax.axis_index("tp")
    z, core = tp // 2, lax.rem(tp, 2)
    n = len(PARTS)
    arrived, sent, (cbuf, in_sem, w_sem, p_send, p_recv, c_send, c_recv) = rest[:2 * n], rest[2 * n:4 * n], rest[4 * n:]
    columns = heads * width
    f32, bf16 = jnp.float32, jnp.bfloat16

    def tp_partner(step, sign=1):
        dz, other = step
        zz = lax.rem(z + (dz if sign > 0 else RING - dz), RING)
        cc = 1 - core if other else core
        return zz * 2 + cc

    barrier = pltpu.get_barrier_semaphore()
    swapped = tp + 1 - 2 * core
    for d in FAR_FIRST[:-1]:
        pl.semaphore_signal(
            barrier, inc=1, device_id={"ctx_1": lax.rem(x + d, RING), "tp": swapped}, device_id_type=MESH
        )
        pl.semaphore_signal(
            barrier, inc=1, device_id={"ctx_0": lax.rem(y + d, RING), "tp": swapped}, device_id_type=MESH
        )
    for step in TP_STEPS:
        pl.semaphore_signal(barrier, inc=1, device_id={"tp": tp_partner(step)}, device_id_type=MESH)

    def weight_copies(l):
        return (
            pltpu.make_async_copy(wq_hbm.at[l], wqkv.at[l, :, pl.ds(0, columns)], w_sem.at[l, 0]),
            pltpu.make_async_copy(wk_hbm.at[l], wqkv.at[l, :, pl.ds(columns, width)], w_sem.at[l, 1]),
            pltpu.make_async_copy(wv_hbm.at[l], wqkv.at[l, :, pl.ds(columns + width, width)], w_sem.at[l, 2]),
        )

    def late_start(l):
        for b in range(batch):
            pltpu.make_async_copy(
                kc_hbm.at[l, b], kcat.at[l, :, pl.ds(b * width, width)], w_sem.at[l, 3]
            ).start()
        pltpu.make_async_copy(vc_hbm.at[l], vcat.at[l], w_sem.at[l, 4]).start()
        pltpu.make_async_copy(wo_hbm.at[l], wo.at[l], w_sem.at[l, 5]).start()

    hidden_copy = pltpu.make_async_copy(hidden_hbm, hidden_v, in_sem.at[0])
    gains_copy = pltpu.make_async_copy(gains_hbm, gains_v, in_sem.at[1])
    lengths_copy = pltpu.make_async_copy(lengths_hbm, lengths, in_sem.at[2])
    lengths_copy.start()
    hidden_copy.start()
    gains_copy.start()
    for copy in weight_copies(0):
        copy.start()

    lengths_copy.wait()
    row = lax.broadcasted_iota(jnp.int32, (batch, width), 0)
    lane = lax.broadcasted_iota(jnp.int32, (batch, width), 1)
    half = width // 2
    length = jnp.zeros((batch, width), jnp.int32)
    for b in range(batch):
        length = jnp.where(row == b, lengths[b], length)
    low = lane < half
    exponents = jnp.where(low, lane, lane - half).astype(f32) * (2.0 / width)
    angles = length.astype(f32) * jnp.exp(-exponents * math.log(ROPE_BASE))
    cosine = jnp.cos(angles)
    sine = jnp.where(low, -jnp.sin(angles), jnp.sin(angles))
    usable = (y * RING + x) * span + lane < length
    scale = 1.0 / math.sqrt(width)
    wide_row = lax.broadcasted_iota(jnp.int32, (2 * batch, batch * width), 0)
    wide_col = lax.broadcasted_iota(jnp.int32, (2 * batch, batch * width), 1)
    own_block = jnp.where(lax.rem(wide_row, batch) == wide_col // width, 1.0, 0.0).astype(bf16)
    for part in range(heads // 2):
        diag[pl.ds(part * 2 * batch, 2 * batch), :] = own_block

    def spread(tall):
        return jnp.concatenate([tall] * batch, axis=1) * diag[...]

    def start(l, p, e):
        axis, me = ("ctx_1", x) if PARTS[p][0] == (e == 0) else ("ctx_0", y)
        for d in FAR_FIRST:
            pltpu.make_async_remote_copy(
                src_ref=sent[2 * p + e].at[l], dst_ref=arrived[2 * p + e].at[l, me],
                send_sem=p_send.at[l, p, e], recv_sem=p_recv.at[l, p, e],
                device_id={axis: lax.rem(me + d, RING), "tp": swapped}, device_id_type=MESH,
            ).start()

    def bytes_of(ref, sem):
        pltpu.make_async_copy(ref, ref, sem).wait()

    def arrive(l, p, e):
        bytes_of(arrived[2 * p + e].at[l], p_recv.at[l, p, e])

    def all_sent(l, parts):
        for p in parts:
            for e in range(2):
                bytes_of(arrived[2 * p + e].at[l], p_send.at[l, p, e])

    def tp_start(l, part):
        for step in TP_STEPS:
            pltpu.make_async_remote_copy(
                src_ref=cbuf.at[l, part, tp], dst_ref=cbuf.at[l, part, tp],
                send_sem=c_send.at[l, part], recv_sem=c_recv.at[l, part],
                device_id={"tp": tp_partner(step)}, device_id_type=MESH,
            ).start()

    def total(l, p, e):
        buf = arrived[2 * p + e]
        return (buf[l, 0] + buf[l, 1]) + (buf[l, 2] + buf[l, 3])

    def tile(values, i):
        return values[:, i * width:(i + 1) * width]

    def over_lane(values, i):
        return jnp.broadcast_to(values[:, i:i + 1], (batch, width))

    def weighted(l, p, e, factors):
        buf = arrived[2 * p + e]
        out = []
        for k, h in enumerate(PARTS[p][1]):
            terms = [
                over_lane(factors[s], h % (heads // 2)) * buf[l, s, :, pl.ds(k * width, width)]
                for s in range(RING)
            ]
            out.append((terms[0] + terms[1]) + (terms[2] + terms[3]))
        return out

    def stats_of(l, p, e):
        at = len(PARTS[p][1]) * width
        return [arrived[2 * p + e][l, s, :, pl.ds(at, width)] for s in range(RING)]

    def put(l, p, e, tiles):
        for k, t in enumerate(tiles):
            sent[2 * p + e][l, :, pl.ds(k * width, width)] = t

    hidden_copy.wait()
    gains_copy.wait()

    def layer(l, stream):
        for copy in weight_copies(l):
            copy.wait()
        if l == 0:
            late_start(0)
            for later in range(1, layers):
                for copy in weight_copies(later):
                    copy.start()
                late_start(later)
        gain = gains_v[pl.ds(l, 1), :].astype(f32)
        scaled = (stream * gain).astype(bf16)
        squares = stream * stream
        squares = functools.reduce(jnp.add, [tile(squares, i) for i in range(features // width)])
        products = [
            jnp.dot(scaled, wqkv[l, :, pl.ds(hs[0] * width, len(hs) * width)], preferred_element_type=f32)
            for _, hs, _ in A_PARTS
        ]
        a_ids, b_ids = range(len(A_PARTS)), range(len(A_PARTS), n)
        for p in a_ids:
            sent[2 * p][l, :, pl.ds(0, 2 * width)] = products[p]
            if PARTS[p][2]:
                sent[2 * p][l, :, pl.ds(2 * width, width)] = squares
            if l == 0 and p == 0:
                pl.semaphore_wait(barrier, 2 * (RING - 1) + len(TP_STEPS))
            start(l, p, 0)
        for p in a_ids:
            arrive(l, p, 0)
            sent[2 * p + 1][l] = total(l, p, 0)
            start(l, p, 1)

        query = [None] * heads
        for p in a_ids[:-1]:
            arrive(l, p, 1)
            raw = total(l, p, 1)
            if PARTS[p][2]:
                mean = jnp.sum(tile(raw, 2), axis=1, keepdims=True) / (RING * RING * features)
                inverse = jnp.broadcast_to(lax.rsqrt(mean + NORM_EPS), (batch, width))
                turn_cos, turn_sin = cosine * inverse, sine * inverse
            for k, h in enumerate(PARTS[p][1]):
                u = tile(raw, k)
                query[h] = (u * turn_cos + pltpu.roll(u, half, axis=1) * turn_sin).astype(bf16)
        tall = jnp.concatenate(query, axis=0)
        bytes_of(kcat.at[l], w_sem.at[l, 3])
        scores = lax.dot_general(
            spread(tall), kcat[l], (((1,), (1,)), ((), ())), preferred_element_type=f32
        ) * scale
        group = heads // 2
        stats = [jnp.zeros((batch, width), f32)] * 2
        weights = []
        for h in range(heads):
            masked = jnp.where(usable, scores[h * batch:(h + 1) * batch], MASK_FILL)
            top = jnp.max(masked, axis=1, keepdims=True)
            weight = jnp.where(usable, jnp.exp(masked - top), 0.0)
            amount = jnp.sum(weight, axis=1, keepdims=True)
            weights.append(weight.astype(bf16))
            i = h % group
            stats[h // group] = jnp.where(
                lane == i, top, jnp.where(lane == half + i, amount, stats[h // group])
            )
        bytes_of(vcat.at[l], w_sem.at[l, 4])
        sums = jnp.dot(
            spread(jnp.concatenate(weights, axis=0)), vcat[l], preferred_element_type=f32
        )
        for p in b_ids:
            _, hs, more = PARTS[p]
            put(l, p, 0, [sums[h * batch:(h + 1) * batch] for h in hs] + [stats[hs[0] // group]] * more)
            start(l, p, 0)

        p = a_ids[-1]
        arrive(l, p, 1)
        raw = total(l, p, 1)
        u = tile(raw, 0)
        new_key = (u * turn_cos + pltpu.roll(u, half, axis=1) * turn_sin).astype(bf16).astype(f32)
        new_value = (tile(raw, 1) * inverse).astype(bf16).astype(f32)
        own = []
        for g in range(2):
            packed = jnp.where(lane >= half, 1.0, 0.0)
            for i in range(group):
                match = jnp.sum(query[g * group + i].astype(f32) * new_key, axis=1, keepdims=True)
                packed = jnp.where(lane == i, match * scale, packed)
            own.append(packed)
        all_sent(l, a_ids)
        bytes_of(wo.at[l], w_sem.at[l, 5])

        shrink = [None, None]
        for p in b_ids:
            arrive(l, p, 0)
            _, hs, more = PARTS[p]
            g = hs[0] // group
            tiles = []
            if more:
                each = stats_of(l, p, 0)
                top = functools.reduce(jnp.maximum, each)
                shrink[g] = [jnp.exp(t - top) for t in each]
                amount = functools.reduce(
                    jnp.add, [pltpu.roll(e, half, axis=1) * t for e, t in zip(shrink[g], each)]
                )
                tiles = [jnp.where(low, top, amount)]
            put(l, p, 1, weighted(l, p, 0, shrink[g]) + tiles)
            start(l, p, 1)

        share = [None, None]
        out = [None] * C_PARTS
        piece = features // C_PARTS
        for p in b_ids:
            arrive(l, p, 1)
            _, hs, more = PARTS[p]
            g = hs[0] // group
            if more:
                each = stats_of(l, p, 1) + [own[g]]
                top = functools.reduce(jnp.maximum, each)
                factors = [jnp.exp(t - top) for t in each]
                amount = functools.reduce(
                    jnp.add, [e * pltpu.roll(t, half, axis=1) for e, t in zip(factors, each)]
                )
                share[g] = [e / amount for e in factors]
            context = [
                v + over_lane(share[g][RING], h % group) * new_value
                for v, h in zip(weighted(l, p, 1, share[g]), hs)
            ]
            context = jnp.concatenate(context, axis=1).astype(bf16)
            for c in range(C_PARTS):
                product = jnp.dot(
                    context, wo[l, pl.ds(hs[0] * width, len(hs) * width), pl.ds(c * piece, piece)],
                    preferred_element_type=f32,
                )
                out[c] = product if out[c] is None else out[c] + product
        for c in range(C_PARTS):
            cbuf[l, c, tp] = out[c]
            tp_start(l, c)
        all_sent(l, b_ids)
        pieces = []
        for c in range(C_PARTS):
            bytes_of(cbuf.at[l, c, pl.ds(0, len(TP_STEPS))], c_recv.at[l, c])
            t = [cbuf[l, c, i] for i in range(2 * RING)]
            pieces.append(((t[0] + t[1]) + (t[2] + t[3])) + ((t[4] + t[5]) + (t[6] + t[7])))
        stream = stream + jnp.concatenate(pieces, axis=1)
        for c in range(C_PARTS):
            bytes_of(cbuf.at[l, c, pl.ds(0, len(TP_STEPS))], c_send.at[l, c])
        return stream

    stream = hidden_v[...].astype(f32)
    for l in range(layers):
        stream = layer(l, stream)
    out_ref[...] = stream


def on_device(hidden, norm_gains, w_query, w_key, w_value, w_out, key_cache, value_cache, lengths):
    layers, features, columns = w_query.shape
    batch, _, span, width = key_cache.shape[1:]
    heads = columns // width
    keys = key_cache.reshape(layers, batch, span, width)
    values = value_cache.reshape(layers, batch * span, width)
    f32, bf16 = jnp.float32, jnp.bfloat16
    messages = [(len(hs) + more) * width for _, hs, more in PARTS for _ in range(2)]
    return pl.pallas_call(
        functools.partial(kernel, layers, batch, heads, width, span, features),
        out_shape=jax.ShapeDtypeStruct((batch, features), f32),
        in_specs=[pl.BlockSpec(memory_space=pltpu.HBM)] * 9,
        out_specs=pl.BlockSpec(memory_space=pltpu.VMEM),
        scratch_shapes=[
            pltpu.SMEM((batch,), jnp.int32),
            pltpu.VMEM((batch, features), bf16),
            pltpu.VMEM((layers, features), bf16),
            pltpu.VMEM((layers, features, columns + 2 * width), bf16),
            pltpu.VMEM((layers, columns, features), bf16),
            pltpu.VMEM((layers, span, batch * width), bf16),
            pltpu.VMEM((layers, batch * span, width), bf16),
            pltpu.VMEM((heads * batch, batch * width), bf16),
            *[pltpu.VMEM((layers, RING, batch, w), f32) for w in messages],
            *[pltpu.VMEM((layers, batch, w), f32) for w in messages],
            pltpu.VMEM((layers, C_PARTS, 2 * RING, batch, features // C_PARTS), f32),
            pltpu.SemaphoreType.DMA((3,)),
            pltpu.SemaphoreType.DMA((layers, 6)),
            pltpu.SemaphoreType.DMA((layers, len(PARTS), 2)),
            pltpu.SemaphoreType.DMA((layers, len(PARTS), 2)),
            pltpu.SemaphoreType.DMA((layers, C_PARTS)),
            pltpu.SemaphoreType.DMA((layers, C_PARTS)),
        ],
        compiler_params=pltpu.CompilerParams(
            collective_id=0, has_side_effects=True, vmem_limit_bytes=48 * 1024 * 1024
        ),
    )(*[pltpu.with_memory_space_constraint(a, pltpu.HBM) for a in (hidden, norm_gains, w_query, w_key, w_value, w_out, keys, values, lengths)])


def solution(mesh):
    finer = Mesh(mesh.devices.reshape(RING, RING, mesh.shape["tp"]), CTX + ("tp",))
    return jax.shard_map(
        on_device,
        mesh=finer,
        in_specs=(
            P(None, CTX),
            P(None, CTX),
            P(None, CTX, "tp"),
            P(None, CTX, "tp"),
            P(None, CTX, "tp"),
            P(None, "tp", CTX),
            P(None, None, "tp", CTX, None),
            P(None, None, "tp", CTX, None),
            P(),
        ),
        out_specs=P(None, CTX),
        check_vma=False,
    )
```

time: 87.5 us -> 85 us (0.971)
  Pallas kernels: 86.8 us -> 84.3 us
    pallas_call x1, Pallas kernels: 86.8 us -> 84.3 us  [on_device(): pl.pallas_call(functools.partial(kernel, layers, batch, heads, width, spa...]
where the time goes in v3:
time: 85 us; the launch traced here: 84.9 us
  Pallas kernels  84.3 us (99%)
    pallas_call x1, Pallas kernels, on_device(): pl.pallas_call(functools.partial(kernel, layers, batch, heads, width, spa...  84.3 us

profile of v3, /device:TPU:1, one launch (start us, length us, event | category | flops | bytes accessed | tf_op | source)
XLA Modules:
  0.0 84.9 jit_solution(3947547007622986195)
XLA Ops:
  0.0 84.3 %shard_map.91 = f32[8,512]{1,0:T(8,128)S(1)} custom-call(bf16[8,512]{1,0:T(8,128)(2,1)} %hidden_hbm.1, bf16[4,512]{1,0:T(4,128)(2,1)} %gains_hbm.1, bf16[4,512,1024]{2,1,0:T(8,128)(2,1)} %wq_hbm.1, bf16[4,512,128]{2,1,0:T(8,128)(2,1)} %wk_hbm.1, bf16[4,512,128]{2,1,0:T(8,128)(2,1)} %wv_hbm.1, bf16[4,1024,512]{2,1,0:T(8,128)(2,1)} %wo_hbm.1, ...), custom_call_target="tpu_custom_call" | custom-call | tf_op jit(solution)/shard_map/pallas_call | solution.py:322
  84.3 0.6 copy.11

commit v4 on v3

--- a/solution.py
+++ b/solution.py
@@ -17,17 +17,17 @@
 RING = 4
 FAR_FIRST = (2, 1, 3, 0)
 TP_STEPS = ((2, 0), (2, 1), (1, 0), (1, 1), (3, 0), (3, 1), (0, 1))
-A_PARTS = ((True, (0, 1), 1), (False, (4, 5), 0), (True, (2, 3), 0), (False, (6, 7), 0), (False, (8, 9), 0))
+A_PARTS = ((True, (0, 1), 1), (False, (2, 3, 4), 0), (True, (5, 6, 7), 0), (False, (8, 9), 0))
 B_PARTS = ((True, (0, 1), 1), (False, (4, 5), 1), (True, (2, 3), 0), (False, (6, 7), 0))
 PARTS = A_PARTS + B_PARTS
-C_PARTS = 2
+C_PARTS = 1
 
 
 def kernel(
     layers, batch, heads, width, span, features,
     hidden_hbm, gains_hbm, wq_hbm, wk_hbm, wv_hbm, wo_hbm, kc_hbm, vc_hbm, lengths_hbm,
     out_ref,
-    lengths, hidden_v, gains_v, wqkv, wo, kcat, vcat, diag,
+    lengths, hidden_v, gains_v, wqkv, wo, kcat, vcat, turned, diag,
     *rest,
 ):
     y = lax.axis_index("ctx_0")
@@ -35,7 +35,7 @@
     tp = lax.axis_index("tp")
     z, core = tp // 2, lax.rem(tp, 2)
     n = len(PARTS)
-    arrived, sent, (cbuf, in_sem, w_sem, p_send, p_recv, c_send, c_recv) = rest[:2 * n], rest[2 * n:4 * n], rest[4 * n:]
+    arrived, sent, (cbuf, in_sem, w_sem, wq_sem, p_send, p_recv, c_send, c_recv) = rest[:2 * n], rest[2 * n:4 * n], rest[4 * n:]
     columns = heads * width
     f32, bf16 = jnp.float32, jnp.bfloat16
 
@@ -58,11 +58,14 @@
         pl.semaphore_signal(barrier, inc=1, device_id={"tp": tp_partner(step)}, device_id_type=MESH)
 
     def weight_copies(l):
-        return (
-            pltpu.make_async_copy(wq_hbm.at[l], wqkv.at[l, :, pl.ds(0, columns)], w_sem.at[l, 0]),
+        copies = []
+        for p, (_, hs, _) in enumerate(A_PARTS[:-1]):
+            at = pl.ds(hs[0] * width, len(hs) * width)
+            copies.append(pltpu.make_async_copy(wq_hbm.at[l, :, at], wqkv.at[l, :, at], wq_sem.at[l, p]))
+        return copies + [
             pltpu.make_async_copy(wk_hbm.at[l], wqkv.at[l, :, pl.ds(columns, width)], w_sem.at[l, 1]),
             pltpu.make_async_copy(wv_hbm.at[l], wqkv.at[l, :, pl.ds(columns + width, width)], w_sem.at[l, 2]),
-        )
+        ]
 
     def late_start(l):
         for b in range(batch):
@@ -75,11 +78,11 @@
     hidden_copy = pltpu.make_async_copy(hidden_hbm, hidden_v, in_sem.at[0])
     gains_copy = pltpu.make_async_copy(gains_hbm, gains_v, in_sem.at[1])
     lengths_copy = pltpu.make_async_copy(lengths_hbm, lengths, in_sem.at[2])
-    lengths_copy.start()
     hidden_copy.start()
     gains_copy.start()
     for copy in weight_copies(0):
         copy.start()
+    lengths_copy.start()
 
     lengths_copy.wait()
     row = lax.broadcasted_iota(jnp.int32, (batch, width), 0)
@@ -165,34 +168,41 @@
     gains_copy.wait()
 
     def layer(l, stream):
-        for copy in weight_copies(l):
-            copy.wait()
-        if l == 0:
-            late_start(0)
-            for later in range(1, layers):
-                for copy in weight_copies(later):
-                    copy.start()
-                late_start(later)
+        copies = weight_copies(l)
+        if l > 0:
+            for copy in copies:
+                copy.wait()
         gain = gains_v[pl.ds(l, 1), :].astype(f32)
         scaled = (stream * gain).astype(bf16)
         squares = stream * stream
         squares = functools.reduce(jnp.add, [tile(squares, i) for i in range(features // width)])
-        products = [
-            jnp.dot(scaled, wqkv[l, :, pl.ds(hs[0] * width, len(hs) * width)], preferred_element_type=f32)
-            for _, hs, _ in A_PARTS
-        ]
+        products = []
+        for p, (_, hs, _) in enumerate(A_PARTS):
+            if l == 0:
+                for copy in copies[p:p + 1] if p < len(A_PARTS) - 1 else copies[p:]:
+                    copy.wait()
+            products.append(
+                jnp.dot(scaled, wqkv[l, :, pl.ds(hs[0] * width, len(hs) * width)], preferred_element_type=f32)
+            )
         a_ids, b_ids = range(len(A_PARTS)), range(len(A_PARTS), n)
         for p in a_ids:
-            sent[2 * p][l, :, pl.ds(0, 2 * width)] = products[p]
+            sent[2 * p][l, :, pl.ds(0, len(PARTS[p][1]) * width)] = products[p]
             if PARTS[p][2]:
                 sent[2 * p][l, :, pl.ds(2 * width, width)] = squares
             if l == 0 and p == 0:
                 pl.semaphore_wait(barrier, 2 * (RING - 1) + len(TP_STEPS))
             start(l, p, 0)
+        if l == 0:
+            late_start(0)
         for p in a_ids:
             arrive(l, p, 0)
             sent[2 * p + 1][l] = total(l, p, 0)
             start(l, p, 1)
+        if l + 1 < layers:
+            for copy in weight_copies(l + 1):
+                copy.start()
+        bytes_of(kcat.at[l], w_sem.at[l, 3])
+        turned[...] = kcat[l].T
 
         query = [None] * heads
         for p in a_ids[:-1]:
@@ -206,9 +216,8 @@
                 u = tile(raw, k)
                 query[h] = (u * turn_cos + pltpu.roll(u, half, axis=1) * turn_sin).astype(bf16)
         tall = jnp.concatenate(query, axis=0)
-        bytes_of(kcat.at[l], w_sem.at[l, 3])
         scores = lax.dot_general(
-            spread(tall), kcat[l], (((1,), (1,)), ((), ())), preferred_element_type=f32
+            spread(tall), turned[...], (((1,), (0,)), ((), ())), preferred_element_type=f32
         ) * scale
         group = heads // 2
         stats = [jnp.zeros((batch, width), f32)] * 2
@@ -231,6 +240,9 @@
             _, hs, more = PARTS[p]
             put(l, p, 0, [sums[h * batch:(h + 1) * batch] for h in hs] + [stats[hs[0] // group]] * more)
             start(l, p, 0)
+
+        if l + 1 < layers:
+            late_start(l + 1)
 
         p = a_ids[-1]
         arrive(l, p, 1)
@@ -332,12 +344,14 @@
             pltpu.VMEM((layers, columns, features), bf16),
             pltpu.VMEM((layers, span, batch * width), bf16),
             pltpu.VMEM((layers, batch * span, width), bf16),
+            pltpu.VMEM((batch * width, span), bf16),
             pltpu.VMEM((heads * batch, batch * width), bf16),
             *[pltpu.VMEM((layers, RING, batch, w), f32) for w in messages],
             *[pltpu.VMEM((layers, batch, w), f32) for w in messages],
             pltpu.VMEM((layers, C_PARTS, 2 * RING, batch, features // C_PARTS), f32),
             pltpu.SemaphoreType.DMA((3,)),
             pltpu.SemaphoreType.DMA((layers, 6)),
+            pltpu.SemaphoreType.DMA((layers, len(A_PARTS) - 1)),
             pltpu.SemaphoreType.DMA((layers, len(PARTS), 2)),
             pltpu.SemaphoreType.DMA((layers, len(PARTS), 2)),
             pltpu.SemaphoreType.DMA((layers, C_PARTS)),

time: 85 us -> 83.9 us (0.987)
  Pallas kernels: 84.3 us -> 83.1 us
    pallas_call x1, Pallas kernels: 84.3 us -> 83.1 us  [on_device(): pl.pallas_call(functools.partial(kernel, layers, batch, heads, width, spa...]
where the time goes in v4:
time: 83.9 us; the launch traced here: 83.7 us
  Pallas kernels  83.1 us (99%)
    pallas_call x1, Pallas kernels, on_device(): pl.pallas_call(functools.partial(kernel, layers, batch, heads, width, spa...  83.1 us

profile of v4, /device:TPU:1, one launch (start us, length us, event | category | flops | bytes accessed | tf_op | source)
XLA Modules:
  0.0 83.7 jit_solution(6082718605582775237)
XLA Ops:
  0.0 83.1 %shard_map.91 = f32[8,512]{1,0:T(8,128)S(1)} custom-call(bf16[8,512]{1,0:T(8,128)(2,1)} %hidden_hbm.1, bf16[4,512]{1,0:T(4,128)(2,1)} %gains_hbm.1, bf16[4,512,1024]{2,1,0:T(8,128)(2,1)} %wq_hbm.1, bf16[4,512,128]{2,1,0:T(8,128)(2,1)} %wk_hbm.1, bf16[4,512,128]{2,1,0:T(8,128)(2,1)} %wv_hbm.1, bf16[4,1024,512]{2,1,0:T(8,128)(2,1)} %wo_hbm.1, ...), custom_call_target="tpu_custom_call" | custom-call | tf_op jit(solution)/shard_map/pallas_call | solution.py:334
  83.1 0.6 copy.11

commit v5 on v4

--- a/solution.py
+++ b/solution.py
@@ -17,8 +17,8 @@
 RING = 4
 FAR_FIRST = (2, 1, 3, 0)
 TP_STEPS = ((2, 0), (2, 1), (1, 0), (1, 1), (3, 0), (3, 1), (0, 1))
-A_PARTS = ((True, (0, 1), 1), (False, (2, 3, 4), 0), (True, (5, 6, 7), 0), (False, (8, 9), 0))
-B_PARTS = ((True, (0, 1), 1), (False, (4, 5), 1), (True, (2, 3), 0), (False, (6, 7), 0))
+A_PARTS = ((False, (0, 1), 1), (True, (2, 3, 4), 0), (False, (5, 6, 7), 0), (True, (8, 9), 0))
+B_PARTS = ((False, (0, 1), 1), (True, (4, 5), 1), (False, (2, 3), 0), (True, (6, 7), 0))
 PARTS = A_PARTS + B_PARTS
 C_PARTS = 1
 
@@ -128,11 +128,12 @@
                 bytes_of(arrived[2 * p + e].at[l], p_send.at[l, p, e])
 
     def tp_start(l, part):
-        for step in TP_STEPS:
+        partners = [lax.rem(z + dz, RING) * 2 + to for dz in (2, 1, 3) for to in (0, 1)] + [swapped]
+        for partner in partners:
             pltpu.make_async_remote_copy(
                 src_ref=cbuf.at[l, part, tp], dst_ref=cbuf.at[l, part, tp],
                 send_sem=c_send.at[l, part], recv_sem=c_recv.at[l, part],
-                device_id={"tp": tp_partner(step)}, device_id_type=MESH,
+                device_id={"tp": partner}, device_id_type=MESH,
             ).start()
 
     def total(l, p, e):

time: 83.9 us -> 82.8 us (0.987)
  Pallas kernels: 83.1 us -> 82.1 us
    pallas_call x1, Pallas kernels: 83.1 us -> 82.1 us  [on_device(): pl.pallas_call(functools.partial(kernel, layers, batch, heads, width, spa...]
where the time goes in v5:
time: 82.8 us; the launch traced here: 82.7 us
  Pallas kernels  82.1 us (99%)
    pallas_call x1, Pallas kernels, on_device(): pl.pallas_call(functools.partial(kernel, layers, batch, heads, width, spa...  82.1 us

profile of v5, /device:TPU:1, one launch (start us, length us, event | category | flops | bytes accessed | tf_op | source)
XLA Modules:
  0.0 82.7 jit_solution(4717510442562036998)
XLA Ops:
  0.0 82.1 %shard_map.91 = f32[8,512]{1,0:T(8,128)S(1)} custom-call(bf16[8,512]{1,0:T(8,128)(2,1)} %hidden_hbm.1, bf16[4,512]{1,0:T(4,128)(2,1)} %gains_hbm.1, bf16[4,512,1024]{2,1,0:T(8,128)(2,1)} %wq_hbm.1, bf16[4,512,128]{2,1,0:T(8,128)(2,1)} %wk_hbm.1, bf16[4,512,128]{2,1,0:T(8,128)(2,1)} %wv_hbm.1, bf16[4,1024,512]{2,1,0:T(8,128)(2,1)} %wo_hbm.1, ...), custom_call_target="tpu_custom_call" | custom-call | tf_op jit(solution)/shard_map/pallas_call | solution.py:335
  82.1 0.6 copy.11

commit v6 on v5

--- a/solution.py
+++ b/solution.py
@@ -225,8 +225,8 @@
         weights = []
         for h in range(heads):
             masked = jnp.where(usable, scores[h * batch:(h + 1) * batch], MASK_FILL)
-            top = jnp.max(masked, axis=1, keepdims=True)
-            weight = jnp.where(usable, jnp.exp(masked - top), 0.0)
+            top = jnp.maximum(jnp.max(masked, axis=1, keepdims=True), 0.1 * MASK_FILL)
+            weight = jnp.exp(masked - top)
             amount = jnp.sum(weight, axis=1, keepdims=True)
             weights.append(weight.astype(bf16))
             i = h % group

time: 82.8 us -> 82.8 us (level)
  no operation moved by 1% of the time
where the time goes in v6:
time: 82.8 us; the launch traced here: 82.7 us
  Pallas kernels  82.1 us (99%)
    pallas_call x1, Pallas kernels, on_device(): pl.pallas_call(functools.partial(kernel, layers, batch, heads, width, spa...  82.1 us

profile of v6, /device:TPU:1, one launch (start us, length us, event | category | flops | bytes accessed | tf_op | source)
XLA Modules:
  0.0 82.7 jit_solution(17969058537282239670)
XLA Ops:
  0.0 82.1 %shard_map.91 = f32[8,512]{1,0:T(8,128)S(1)} custom-call(bf16[8,512]{1,0:T(8,128)(2,1)} %hidden_hbm.1, bf16[4,512]{1,0:T(4,128)(2,1)} %gains_hbm.1, bf16[4,512,1024]{2,1,0:T(8,128)(2,1)} %wq_hbm.1, bf16[4,512,128]{2,1,0:T(8,128)(2,1)} %wk_hbm.1, bf16[4,512,128]{2,1,0:T(8,128)(2,1)} %wv_hbm.1, bf16[4,1024,512]{2,1,0:T(8,128)(2,1)} %wo_hbm.1, ...), custom_call_target="tpu_custom_call" | custom-call | tf_op jit(solution)/shard_map/pallas_call | solution.py:335
  82.1 0.6 copy.11
